TPU v7x, 16 devices: a whole 2x2x2 slice. The times are simulated.
16 devices in a mesh: rep: 4 (over z, y), data: 4 (over x, core).
Axes of the slice: x: 2, y: 2, z: 2, core: 2. Of those that a mesh axis runs over, the one named last changes fastest.
Arguments:
- hidden: bfloat16 [8192, 3584], P(('rep', 'data')), parts along dimension 0
- adapter_id: int32 [8192], P(('rep', 'data')), parts along dimension 0
- w_gate: bfloat16 [3584, 18944], replicated
- w_up: bfloat16 [3584, 18944], replicated
- w_down: bfloat16 [18944, 3584], replicated
- a_gate: bfloat16 [128, 3584, 16], replicated
- b_gate: bfloat16 [128, 16, 18944], P('data')
- a_up: bfloat16 [128, 3584, 16], replicated
- b_up: bfloat16 [128, 16, 18944], P('data')
- a_down: bfloat16 [128, 18944, 16], replicated
- b_down: bfloat16 [128, 16, 3584], P('data')
Outputs:
- output: bfloat16 [8192, 3584], P(('rep', 'data')), parts along dimension 0
There are 4 independent parts. A program takes and returns all parts, laid end to end along the dimension named above; an argument that names none is the same for every part.
All inputs are finite; a program needn't handle non-finite values.
Results may differ from a plain program's by a relative error of at most 0.0073344.
Values are sent between devices in bfloat16 or wider.
A program may use at most 2.25 GiB of HBM per device.

v0:
```python
import functools

import jax
import jax.numpy as jnp
from jax import lax
from jax.experimental import pallas as pl
from jax.experimental.pallas import tpu as pltpu
from jax.sharding import PartitionSpec as P

LORA_SCALE = 2.0
F32 = jnp.float32
BF16 = jnp.bfloat16
NT = (((1,), (1,)), ((), ()))
VMEM_LIMIT = 62 * 1024 * 1024


def row_counts(tok):
    if tok == 512:
        return (256, 352, 368, 512)
    return (tok // 2, tok)


def per_row_count(rows_ref, counts, body):
    rows = rows_ref[0]
    below = 0
    for count in counts:
        pl.when((rows > below) & (rows <= count))(functools.partial(body, count))
        below = count


def whole(shape):
    zeros = (0,) * len(shape)
    return pl.BlockSpec(shape, lambda *_: zeros, pipeline_mode=pl.Buffered(1))


def low_kernel(counts, rank, info_ref, x_ref, lid_ref, ag_ref, au_ref, lg_ref, lu_ref):
    width = ag_ref.shape[0]
    block = pl.program_id(0)

    def body(m):
        column = block * width + lax.broadcasted_iota(jnp.int32, (m, width), 1)
        mine = (column // rank) == lid_ref[:m, :]
        for a_ref, l_ref in ((ag_ref, lg_ref), (au_ref, lu_ref)):
            low = lax.dot_general(x_ref[:m, :], a_ref[...], NT, preferred_element_type=F32)
            l_ref[:m, :] = jnp.where(mine, low, 0.0).astype(BF16)

    per_row_count(info_ref, counts, body)


def low_rows(info, x, lid, ag, au, own_rows, rank):
    tok, d = x.shape
    width = own_rows // 2
    counts = row_counts(tok)
    spec_a = pl.BlockSpec((width, d), lambda b, info: ((info[1] ^ (b // 2)) * 2 + b % 2, 0))
    spec_l = pl.BlockSpec((tok, width), lambda b, info: (0, b))
    return pl.pallas_call(
        functools.partial(low_kernel, counts, rank),
        grid_spec=pltpu.PrefetchScalarGridSpec(
            num_scalar_prefetch=1,
            grid=(4,),
            in_specs=[whole((tok, d)), whole((tok, 1)), spec_a, spec_a],
            out_specs=[spec_l, spec_l],
        ),
        out_shape=[jax.ShapeDtypeStruct((tok, 4 * width), BF16)] * 2,
        compiler_params=pltpu.CompilerParams(vmem_limit_bytes=VMEM_LIMIT),
        cost_estimate=pl.CostEstimate(flops=2 * 2 * tok * d * 4 * width, bytes_accessed=4 * 4 * width * d, transcendentals=0),
    )(info, x, lid, ag, au)


def mlp_kernel(counts, rank, sub, wide, info_ref, x_ref, lid_ref, lg_ref, lu_ref, wg_ref, wu_ref, bg0_ref, bg1_ref, bu0_ref, bu1_ref,
               wd_ref, a0_ref, a1_ref, bd0_ref, bd1_ref, o_ref, acc_ref, low_ref, ld_ref):
    step = pl.program_id(0)
    tok, d = acc_ref.shape
    half = bg0_ref.shape[0]
    block = wg_ref.shape[1]

    def body(m):
        def branch(at, w_ref, l_ref, b0_ref, b1_ref):
            base = jnp.dot(x_ref[:m, :], w_ref[:, at], preferred_element_type=F32)
            delta = jnp.dot(l_ref[:m, :half], b0_ref[:, at], preferred_element_type=F32)
            delta += jnp.dot(l_ref[:m, half:], b1_ref[:, at], preferred_element_type=F32)
            return base + (LORA_SCALE * delta).astype(BF16).astype(F32)

        @pl.when(step == 0)
        def _():
            acc_ref[:m, :] = jnp.zeros((m, d), F32)
            low_ref[:m, :] = jnp.zeros((m, 2 * half), F32)

        for first in range(0, block, sub):
            at = slice(first, first + sub)
            gate = branch(at, wg_ref, lg_ref, bg0_ref, bg1_ref)
            up = branch(at, wu_ref, lu_ref, bu0_ref, bu1_ref)
            h = (jax.nn.silu(gate) * up).astype(BF16)
            for left in range(0, d, wide):
                to = slice(left, left + wide)
                acc_ref[:m, to] += jnp.dot(h, wd_ref[at, to], preferred_element_type=F32)
            for side, a_ref in ((0, a0_ref), (1, a1_ref)):
                to = slice(side * half, (side + 1) * half)
                low_ref[:m, to] += lax.dot_general(h, a_ref[:, at], NT, preferred_element_type=F32)

        @pl.when(step == pl.num_programs(0) - 1)
        def _():
            column = lax.broadcasted_iota(jnp.int32, (m, 2 * half), 1)
            mine = (column // rank) == lid_ref[:m, :]
            ld_ref[:m, :] = jnp.where(mine, low_ref[:m, :], 0.0).astype(BF16)

            def finish(i, carry):
                to = pl.ds(pl.multiple_of(i * wide, wide), wide)
                delta = jnp.dot(ld_ref[:m, :half], bd0_ref[:, to], preferred_element_type=F32)
                delta += jnp.dot(ld_ref[:m, half:], bd1_ref[:, to], preferred_element_type=F32)
                down = acc_ref[:m, to] + (LORA_SCALE * delta).astype(BF16).astype(F32)
                o_ref[:m, to] = (x_ref[:m, to].astype(F32) + down).astype(BF16)
                return carry

            lax.fori_loop(0, d // wide, finish, 0)
            if m < tok:
                o_ref[m:, :] = jnp.zeros((tok - m, d), BF16)

    per_row_count(info_ref, counts, body)


def mlp(info, x, lid, lg, lu, wg, wu, bg0, bg1, bu0, bu1, wd, ad, bd0, bd1, rank, block=512, sub=256, wide=512):
    tok, d = x.shape
    f = wg.shape[1]
    low = lg.shape[1]
    half = low // 2
    counts = row_counts(tok)
    spec_w = pl.BlockSpec((d, block), lambda i, info: (0, i))
    spec_b = pl.BlockSpec((half, block), lambda i, info: (0, i))
    return pl.pallas_call(
        functools.partial(mlp_kernel, counts, rank, sub, wide),
        grid_spec=pltpu.PrefetchScalarGridSpec(
            num_scalar_prefetch=1,
            grid=(f // block,),
            in_specs=[
                whole((tok, d)), whole((tok, 1)), whole((tok, low)), whole((tok, low)),
                spec_w, spec_w, spec_b, spec_b, spec_b, spec_b,
                pl.BlockSpec((block, d), lambda i, info: (i, 0)),
                pl.BlockSpec((half, block), lambda i, info: (info[1], i)),
                pl.BlockSpec((half, block), lambda i, info: (info[1] ^ 1, i)),
                whole((half, d)), whole((half, d)),
            ],
            out_specs=whole((tok, d)),
            scratch_shapes=[pltpu.VMEM((tok, d), F32), pltpu.VMEM((tok, low), F32), pltpu.VMEM((tok, low), BF16)],
        ),
        out_shape=jax.ShapeDtypeStruct((tok, d), BF16),
        compiler_params=pltpu.CompilerParams(vmem_limit_bytes=VMEM_LIMIT),
        cost_estimate=pl.CostEstimate(flops=6 * tok * (d + low) * f, bytes_accessed=6 * f * (d + low), transcendentals=tok * f),
    )(info, x, lid, lg, lu, wg, wu, bg0, bg1, bu0, bu1, wd, ad, ad, bd0, bd1)


def solution(mesh):
    groups = mesh.shape['data']
    assert groups == 4
    row_spec = P(('rep', 'data'), None)
    tok_spec = P(('rep', 'data'))
    full_two = P(None, None)
    full_three = P(None, None, None)
    owned = P('data', None, None)
    to_chip = [(j, j ^ 2) for j in range(groups)]
    to_core = [(j, j ^ 1) for j in range(groups)]

    def device_fn(hidden, adapter_id, w_gate, w_up, w_down, a_gate, b_gate, a_up, b_up, a_down, b_down):
        tok, d = hidden.shape
        adapters, f, rank = a_down.shape
        per_owner = b_gate.shape[0]
        own_rows = per_owner * rank
        me = lax.axis_index('data').astype(jnp.int32)

        bg0, bu0, bd0 = (b.reshape(own_rows, b.shape[2]) for b in (b_gate, b_up, b_down))
        bg1, bu1, bd1 = (lax.ppermute(b, 'data', to_core) for b in (bg0, bu0, bd0))
        ag, au, ad = (jnp.transpose(a, (0, 2, 1)).reshape(adapters * rank, a.shape[1]) for a in (a_gate, a_up, a_down))

        owner = adapter_id // per_owner
        cross = (owner // 2) != (me // 2)
        lid = ((owner ^ me) & 1) * per_owner + adapter_id % per_owner
        token = jnp.arange(tok, dtype=jnp.int32)
        before = token[None, :] < token[:, None]

        def place(chosen):
            rank_of = jnp.sum((before & chosen[None, :]).astype(jnp.int32), axis=1)
            hot = (token[:, None] == rank_of[None, :]) & chosen[None, :]
            rows = jnp.dot(hot.astype(BF16), hidden, preferred_element_type=F32).astype(BF16)
            lids = jnp.sum(hot.astype(jnp.int32) * (lid[None, :] + 1), axis=1) - 1
            return hot.astype(BF16), rows, lids

        cross_hot, send_x, send_lid = place(cross)
        recv_x = lax.ppermute(send_x, 'data', to_chip)
        recv_lid = lax.ppermute(send_lid, 'data', to_chip)
        stay_hot, stay_x, stay_lid = place(~cross)

        def out_rows(x, lids):
            info = jnp.stack([jnp.sum((lids >= 0).astype(jnp.int32)), me])
            lid_rows = lids[:, None]
            lg, lu = low_rows(info, x, lid_rows, ag, au, own_rows, rank)
            return mlp(info, x, lid_rows, lg, lu, w_gate, w_up, bg0, bg1, bu0, bu1, w_down, ad, bd0, bd1, rank)

        recv_y = out_rows(recv_x, recv_lid)
        back_y = lax.ppermute(recv_y, 'data', to_chip)
        stay_y = out_rows(stay_x, stay_lid)

        pick = (((0,), (0,)), ((), ()))
        out = lax.dot_general(stay_hot, stay_y, pick, preferred_element_type=F32)
        out += lax.dot_general(cross_hot, back_y, pick, preferred_element_type=F32)
        return out.astype(BF16)

    return jax.shard_map(device_fn, mesh=mesh, in_specs=(row_spec, tok_spec, full_two, full_two, full_two, full_three, owned, full_three, owned, full_three, owned), out_specs=row_spec, check_vma=False)
```

profile of v0, /device:TPU:0, one launch (start us, length us, event | category | flops | bytes accessed | tf_op | source)
XLA Modules:
  0.0 623.8 jit_solution(603860352395810554)
XLA Ops:
  0.0 0.7 collective-permute-start
  0.7 0.0 collective-permute-start.1
  0.7 0.7 fusion.23
  1.5 0.0 copy-start.7
  1.5 0.0 copy-start.5
  1.5 0.1 convert_reduce_fusion
  1.6 0.0 copy-start.3
  1.6 0.0 copy-start.9
  1.6 5.9 convolution_convert_fusion
  7.6 3.0 collective-permute-start.4
  10.6 0.0 collective-permute-start.2
  10.6 0.1 convert_reduce_fusion.1
  10.7 0.0 copy-done.9
  10.7 0.0 copy-start.1
  10.8 0.0 copy-done.7
  10.8 0.0 copy-done.3
  10.8 0.5 select_reduce_fusion.1
  11.3 0.0 collective-permute-start.3
  11.4 0.6 broadcast_add_fusion.1
  12.0 0.9 copy.17.lid_ref
  12.9 1.2 pad_add_fusion.info_ref
  14.0 0.0 copy-done.5
  14.0 5.9 convolution_convert_fusion.1.x_ref
  19.9 0.0 copy-done.1
  19.9 11.9 %shard_map.109 = (bf16[512,1024]{1,0:T(8,128)(2,1)}, bf16[512,1024]{1,0:T(8,128)(2,1)}) custom-call(s32[2]{0:T(128)} %pad_add_fusion.info_ref, bf16[512,3584]{1,0:T(8,128)(2,1)} %convolution_convert_fusion.1.x_ref, s32[512,1]{1,0:T(8,128)} %copy.17.lid_ref, bf16[2048,3584]{1,0:T(8,128)(2,1)} %bitcast.21, bf16[2048,3584]{1,0:T(8,128)(2,1)} %bitcast.23), custom_call_target="tpu_custom_call" | custom-call | flops 7516192768 | bytes 14680064 | tf_op jit(solution)/shard_map/pallas_call | solution.py:56
  31.8 58.4 %collective-permute-done.3 = s32[512]{0:T(512)S(1)} collective-permute-done((s32[512]{0:T(512)S(1)}, s32[512]{0:T(512)S(1)}, u32[]{:S(2)}, u32[]{:S(2)}) %collective-permute-start.3) | collective-permute-done | bytes 2080 | tf_op jit(solution)/shard_map/ppermute | solution.py:189
  90.1 0.8 copy.19.lid_ref
  91.0 0.7 convert_reduce_fusion.2
  91.7 1.3 pad_add_fusion.1.info_ref
  93.0 0.0 collective-permute-done.4.x_ref
  93.0 11.7 %shard_map.111 = (bf16[512,1024]{1,0:T(8,128)(2,1)}, bf16[512,1024]{1,0:T(8,128)(2,1)}) custom-call(s32[2]{0:T(128)} %pad_add_fusion.1.info_ref, bf16[512,3584]{1,0:T(8,128)(2,1)} %collective-permute-done.4.x_ref, s32[512,1]{1,0:T(8,128)} %copy.19.lid_ref, bf16[2048,3584]{1,0:T(8,128)(2,1)} %bitcast.22, bf16[2048,3584]{1,0:T(8,128)(2,1)} %bitcast.24), custom_call_target="tpu_custom_call" | custom-call | flops 7516192768 | bytes 14680064 | tf_op jit(solution)/shard_map/pallas_call | solution.py:56
  104.7 0.0 collective-permute-done.2.bd1_ref
  104.7 0.0 collective-permute-done.bg1_ref
  104.7 0.0 collective-permute-done.1.bu1_ref
  104.7 247.1 %shard_map.112 = bf16[512,3584]{1,0:T(8,128)(2,1)} custom-call(s32[2]{0:T(128)} %pad_add_fusion.1.info_ref, bf16[512,3584]{1,0:T(8,128)(2,1)} %collective-permute-done.4.x_ref, s32[512,1]{1,0:T(8,128)} %copy.19.lid_ref, bf16[512,1024]{1,0:T(8,128)(2,1)} %get-tuple-element.11.lg_ref, bf16[512,1024]{1,0:T(8,128)(2,1)} %get-tuple-element.12.lu_ref, ...), custom_call_target="tpu_custom_call" | custom-call | flops 268167020544 | bytes 523763712 | tf_op jit(solution)/shard_map/pallas_call | solution.py:130
  351.8 0.0 collective-permute-start.5
  351.8 0.0 copy-start.4
  351.8 0.0 copy-start.8
  351.8 263.3 %shard_map.110 = bf16[512,3584]{1,0:T(8,128)(2,1)} custom-call(s32[2]{0:T(128)} %pad_add_fusion.info_ref, bf16[512,3584]{1,0:T(8,128)(2,1)} %convolution_convert_fusion.1.x_ref, s32[512,1]{1,0:T(8,128)} %copy.17.lid_ref, bf16[512,1024]{1,0:T(8,128)(2,1)} %get-tuple-element.9.lg_ref, bf16[512,1024]{1,0:T(8,128)(2,1)} %get-tuple-element.10.lu_ref, ...), custom_call_target="tpu_custom_call" | custom-call | flops 268167020544 | bytes 523763712 | tf_op jit(solution)/shard_map/pallas_call | solution.py:130
  615.2 0.0 copy-start
  615.2 0.0 copy-start.2
  615.2 0.0 copy-start.6
  615.2 0.0 collective-permute-done.5
  615.2 0.0 copy-done.4
  615.3 0.0 copy-done.8
  615.3 4.3 fusion.6
  619.6 0.0 copy-done
  619.6 0.0 copy-done.2
  619.6 0.0 copy-done.6
  619.6 4.0 add_convert_fusion
  (2 shorter events, 0.0 us)
Async XLA Ops:
  0.0 104.7 %collective-permute-start = (bf16[512,18944]{1,0:T(8,128)(2,1)}, bf16[512,18944]{1,0:T(8,128)(2,1)}, u32[]{:S(2)}, u32[]{:S(2)}) collective-permute-start(bf16[512,18944]{1,0:T(8,128)(2,1)} %bitcast.27), channel_id=1, source_target_pairs={{0,1},{1,0},{2,3},{3,2},{4,5},{5,4},{6,7},{7,6},{8,9},{9,8},{10,11... | collective-permute-start | bytes 58195976 | tf_op jit(solution)/shard_map/ppermute | solution.py:171
  0.7 103.9 %collective-permute-start.1 = (bf16[512,18944]{1,0:T(8,128)(2,1)}, bf16[512,18944]{1,0:T(8,128)(2,1)}, u32[]{:S(2)}, u32[]{:S(2)}) collective-permute-start(bf16[512,18944]{1,0:T(8,128)(2,1)} %bitcast.30), channel_id=1, source_target_pairs={{0,1},{1,0},{2,3},{3,2},{4,5},{5,4},{6,7},{7,6},{8,9},{9,8},{10,11... | collective-permute-start | bytes 58195976 | tf_op jit(solution)/shard_map/ppermute | solution.py:171
  1.5 9.3 %copy-start.7 = (pred[512]{0:T(512)(128)(4,1)}, pred[512]{0:T(512)(128)(4,1)S(1)}, u32[]{:S(2)}) copy-start(pred[512]{0:T(512)(128)(4,1)S(1)} %get-tuple-element.16) | copy-start | bytes 1540
  1.5 12.6 %copy-start.5 = (pred[512]{0:T(512)(128)(4,1)}, pred[512]{0:T(512)(128)(4,1)S(1)}, u32[]{:S(2)}) copy-start(pred[512]{0:T(512)(128)(4,1)S(1)} %get-tuple-element.15) | copy-start | bytes 1540
  1.6 9.2 %copy-start.3 = (s32[512]{0:T(512)}, s32[512]{0:T(512)S(1)}, u32[]{:S(2)}) copy-start(s32[512]{0:T(512)S(1)} %convert_reduce_fusion) | copy-start | bytes 6148
  1.6 9.1 %copy-start.9 = (s32[512]{0:T(512)S(1)}, s32[512]{0:T(512)}, u32[]{:S(2)}) copy-start(s32[512]{0:T(512)} %param.12) | copy-start | bytes 6148
  7.6 85.4 %collective-permute-start.4 = (bf16[512,3584]{1,0:T(8,128)(2,1)}, bf16[512,3584]{1,0:T(8,128)(2,1)}, u32[]{:S(2)}, u32[]{:S(2)}) collective-permute-start(bf16[512,3584]{1,0:T(8,128)(2,1)} %convolution_convert_fusion), channel_id=1, source_target_pairs={{0,2},{1,3},{2,0},{3,1},{4,6},{5,7},{6,4},{7,5},{8,10},{9,11},{10,... | collective-permute-start | bytes 11010056 | tf_op jit(solution)/shard_map/ppermute | solution.py:188
  10.6 94.1 %collective-permute-start.2 = (bf16[512,3584]{1,0:T(8,128)(2,1)}, bf16[512,3584]{1,0:T(8,128)(2,1)}, u32[]{:S(2)}, u32[]{:S(2)}) collective-permute-start(bf16[512,3584]{1,0:T(8,128)(2,1)} %bitcast.11.bd0_ref), channel_id=1, source_target_pairs={{0,1},{1,0},{2,3},{3,2},{4,5},{5,4},{6,7},{7,6},{8,9},{9,8},{10,11... | collective-permute-start | bytes 11010056 | tf_op jit(solution)/shard_map/ppermute | solution.py:171
  10.7 9.2 %copy-start.1 = (s32[512]{0:T(512)}, s32[512]{0:T(512)S(1)}, u32[]{:S(2)}) copy-start(s32[512]{0:T(512)S(1)} %convert_reduce_fusion.1) | copy-start | bytes 6148
  11.3 78.8 %collective-permute-start.3 = (s32[512]{0:T(512)S(1)}, s32[512]{0:T(512)S(1)}, u32[]{:S(2)}, u32[]{:S(2)}) collective-permute-start(s32[512]{0:T(512)S(1)} %broadcast_add_fusion), channel_id=1, source_target_pairs={{0,2},{1,3},{2,0},{3,1},{4,6},{5,7},{6,4},{7,5},{8,10},{9,11},{10,... | collective-permute-start | bytes 6152 | tf_op jit(solution)/shard_map/ppermute | solution.py:189
  351.8 263.4 %collective-permute-start.5 = (bf16[512,3584]{1,0:T(8,128)(2,1)}, bf16[512,3584]{1,0:T(8,128)(2,1)}, u32[]{:S(2)}, u32[]{:S(2)}) collective-permute-start(bf16[512,3584]{1,0:T(8,128)(2,1)} %shard_map.112), channel_id=1, source_target_pairs={{0,2},{1,3},{2,0},{3,1},{4,6},{5,7},{6,4},{7,5},{8,10},{9,11},{10,... | collective-permute-start | bytes 11010056 | tf_op jit(solution)/shard_map/ppermute | solution.py:199
  351.8 263.4 %copy-start.4 = (s32[512]{0:T(512)S(1)}, s32[512]{0:T(512)}, u32[]{:S(2)}) copy-start(s32[512]{0:T(512)} %copy-done.3) | copy-start | bytes 6148
  351.8 263.4 %copy-start.8 = (pred[512]{0:T(512)(128)(4,1)S(1)}, pred[512]{0:T(512)(128)(4,1)}, u32[]{:S(2)}) copy-start(pred[512]{0:T(512)(128)(4,1)} %copy-done.7) | copy-start | bytes 1540
  615.2 4.4 copy-start
  615.2 4.4 copy-start.2
  615.2 4.4 copy-start.6
where the time goes:
time: 628 us; the launch traced here: 624 us
  Pallas kernels  534 us (85%)
  waiting for transfers between devices  58.4 us (9%)
  matrix products  20.1 us (3%)
    pallas_call x2, Pallas kernels, mlp(): pl.pallas_call(functools.partial(mlp_kernel, counts, rank, sub, wide), gr...  510 us
    ppermute x1, waiting for transfers between devices, device_fn(): recv_lid = lax.ppermute(send_lid, 'data', to_chip)  58.4 us
    pallas_call x2, Pallas kernels, low_rows(): pl.pallas_call(functools.partial(low_kernel, counts, rank), grid_spec=plt...  23.5 us
  transfers between devices with their start and end apart: 6, of which 1 were waited for; matrix products, arithmetic and copies ran while one was open for 3% of the time, Pallas kernels for 46%

commit v1 on v0

--- a/solution.py
+++ b/solution.py
@@ -7,16 +7,18 @@
 from jax.experimental.pallas import tpu as pltpu
 from jax.sharding import PartitionSpec as P
 
+
 LORA_SCALE = 2.0
 F32 = jnp.float32
 BF16 = jnp.bfloat16
 NT = (((1,), (1,)), ((), ()))
 VMEM_LIMIT = 62 * 1024 * 1024
+BLOCK = 512
 
 
 def row_counts(tok):
     if tok == 512:
-        return (256, 352, 368, 512)
+        return (352, 368, 512)
     return (tok // 2, tok)
 
 
@@ -67,12 +69,25 @@
     )(info, x, lid, ag, au)
 
 
-def mlp_kernel(counts, rank, sub, wide, info_ref, x_ref, lid_ref, lg_ref, lu_ref, wg_ref, wu_ref, bg0_ref, bg1_ref, bu0_ref, bu1_ref,
-               wd_ref, a0_ref, a1_ref, bd0_ref, bd1_ref, o_ref, acc_ref, low_ref, ld_ref):
+def mlp_kernel(counts, rank, sub, wide, resume, final, info_ref, x_ref, lid_ref, lg_ref, lu_ref, wg_ref, wu_ref, bg0_ref, bg1_ref,
+               bu0_ref, bu1_ref, wd_ref, a0_ref, a1_ref, *refs):
+    refs = list(refs)
+    bd0_ref, bd1_ref = (refs.pop(0), refs.pop(0)) if final else (None, None)
+    acc_in, low_in = (refs.pop(0), refs.pop(0)) if resume else (None, None)
+    o_ref = refs.pop(0) if final else None
+    acc_out, low_out = (None, None) if final else (refs.pop(0), refs.pop(0))
+    acc_ref, low_ref, ld_ref, sems = refs
     step = pl.program_id(0)
     tok, d = acc_ref.shape
     half = bg0_ref.shape[0]
     block = wg_ref.shape[1]
+
+    def move(pairs):
+        copies = [pltpu.make_async_copy(src, dst, sems.at[i]) for i, (src, dst) in enumerate(pairs)]
+        for copy in copies:
+            copy.start()
+        for copy in copies:
+            copy.wait()
 
     def body(m):
         def branch(at, w_ref, l_ref, b0_ref, b1_ref):
@@ -83,13 +98,16 @@
 
         @pl.when(step == 0)
         def _():
-            acc_ref[:m, :] = jnp.zeros((m, d), F32)
-            low_ref[:m, :] = jnp.zeros((m, 2 * half), F32)
-
-        for first in range(0, block, sub):
-            at = slice(first, first + sub)
-            gate = branch(at, wg_ref, lg_ref, bg0_ref, bg1_ref)
-            up = branch(at, wu_ref, lu_ref, bu0_ref, bu1_ref)
+            if resume:
+                move(((acc_in, acc_ref), (low_in, low_ref)))
+            else:
+                acc_ref[:m, :] = jnp.zeros((m, d), F32)
+                low_ref[:m, :] = jnp.zeros((m, 2 * half), F32)
+
+        def gate_up(at):
+            return at, branch(at, wg_ref, lg_ref, bg0_ref, bg1_ref), branch(at, wu_ref, lu_ref, bu0_ref, bu1_ref)
+
+        def add_down(at, gate, up):
             h = (jax.nn.silu(gate) * up).astype(BF16)
             for left in range(0, d, wide):
                 to = slice(left, left + wide)
@@ -98,8 +116,19 @@
                 to = slice(side * half, (side + 1) * half)
                 low_ref[:m, to] += lax.dot_general(h, a_ref[:, at], NT, preferred_element_type=F32)
 
+        waiting = None
+        for first in range(0, block, sub):
+            now = gate_up(slice(first, first + sub))
+            if waiting is not None:
+                add_down(*waiting)
+            waiting = now
+        add_down(*waiting)
+
         @pl.when(step == pl.num_programs(0) - 1)
         def _():
+            if not final:
+                move(((acc_ref, acc_out), (low_ref, low_out)))
+                return
             column = lax.broadcasted_iota(jnp.int32, (m, 2 * half), 1)
             mine = (column // rank) == lid_ref[:m, :]
             ld_ref[:m, :] = jnp.where(mine, low_ref[:m, :], 0.0).astype(BF16)
@@ -119,34 +148,46 @@
     per_row_count(info_ref, counts, body)
 
 
-def mlp(info, x, lid, lg, lu, wg, wu, bg0, bg1, bu0, bu1, wd, ad, bd0, bd1, rank, block=512, sub=256, wide=512):
+def mlp(info, x, lid, lg, lu, wg, wu, bs, wd, ad, bd, rank, first, stop, sums=None, block=BLOCK, sub=256, wide=512):
     tok, d = x.shape
-    f = wg.shape[1]
     low = lg.shape[1]
     half = low // 2
     counts = row_counts(tok)
-    spec_w = pl.BlockSpec((d, block), lambda i, info: (0, i))
-    spec_b = pl.BlockSpec((half, block), lambda i, info: (0, i))
+    resume, final = sums is not None, bd is not None
+    spec_w = pl.BlockSpec((d, block), lambda i, info: (0, i + first))
+    any_spec = pl.BlockSpec(memory_space=pl.ANY)
+    in_specs = [
+        whole((tok, d)), whole((tok, 1)), whole((tok, low)), whole((tok, low)), spec_w, spec_w,
+        *(pl.BlockSpec((half, block), lambda i, info, off=0 if local else first: (0, i + off)) for _, local in bs),
+        pl.BlockSpec((block, d), lambda i, info: (i + first, 0)),
+        pl.BlockSpec((half, block), lambda i, info: (info[1], i + first)),
+        pl.BlockSpec((half, block), lambda i, info: (info[1] ^ 1, i + first)),
+    ]
+    args = [x, lid, lg, lu, wg, wu, *(b for b, _ in bs), wd, ad, ad]
+    if final:
+        in_specs += [whole((half, d))] * 2
+        args += bd
+        out_specs, out_shape = whole((tok, d)), jax.ShapeDtypeStruct((tok, d), BF16)
+    else:
+        out_specs = [any_spec] * 2
+        out_shape = [jax.ShapeDtypeStruct((tok, d), F32), jax.ShapeDtypeStruct((tok, low), F32)]
+    if resume:
+        in_specs += [any_spec] * 2
+        args += sums
+    width = (stop - first) * block
     return pl.pallas_call(
-        functools.partial(mlp_kernel, counts, rank, sub, wide),
+        functools.partial(mlp_kernel, counts, rank, sub, wide, resume, final),
         grid_spec=pltpu.PrefetchScalarGridSpec(
             num_scalar_prefetch=1,
-            grid=(f // block,),
-            in_specs=[
-                whole((tok, d)), whole((tok, 1)), whole((tok, low)), whole((tok, low)),
-                spec_w, spec_w, spec_b, spec_b, spec_b, spec_b,
-                pl.BlockSpec((block, d), lambda i, info: (i, 0)),
-                pl.BlockSpec((half, block), lambda i, info: (info[1], i)),
-                pl.BlockSpec((half, block), lambda i, info: (info[1] ^ 1, i)),
-                whole((half, d)), whole((half, d)),
-            ],
-            out_specs=whole((tok, d)),
-            scratch_shapes=[pltpu.VMEM((tok, d), F32), pltpu.VMEM((tok, low), F32), pltpu.VMEM((tok, low), BF16)],
+            grid=(stop - first,),
+            in_specs=in_specs,
+            out_specs=out_specs,
+            scratch_shapes=[pltpu.VMEM((tok, d), F32), pltpu.VMEM((tok, low), F32), pltpu.VMEM((tok, low), BF16), pltpu.SemaphoreType.DMA((2,))],
         ),
-        out_shape=jax.ShapeDtypeStruct((tok, d), BF16),
+        out_shape=out_shape,
         compiler_params=pltpu.CompilerParams(vmem_limit_bytes=VMEM_LIMIT),
-        cost_estimate=pl.CostEstimate(flops=6 * tok * (d + low) * f, bytes_accessed=6 * f * (d + low), transcendentals=tok * f),
-    )(info, x, lid, lg, lu, wg, wu, bg0, bg1, bu0, bu1, wd, ad, ad, bd0, bd1)
+        cost_estimate=pl.CostEstimate(flops=6 * tok * (d + low) * width if final else 1000, bytes_accessed=6 * width * (d + low), transcendentals=tok * width),
+    )(info, *args)
 
 
 def solution(mesh):
@@ -161,14 +202,17 @@
     to_core = [(j, j ^ 1) for j in range(groups)]
 
     def device_fn(hidden, adapter_id, w_gate, w_up, w_down, a_gate, b_gate, a_up, b_up, a_down, b_down):
-        tok, d = hidden.shape
+        tok, _ = hidden.shape
         adapters, f, rank = a_down.shape
         per_owner = b_gate.shape[0]
         own_rows = per_owner * rank
         me = lax.axis_index('data').astype(jnp.int32)
 
+        blocks = f // BLOCK
+        early = max(1, blocks // 3)
+
         bg0, bu0, bd0 = (b.reshape(own_rows, b.shape[2]) for b in (b_gate, b_up, b_down))
-        bg1, bu1, bd1 = (lax.ppermute(b, 'data', to_core) for b in (bg0, bu0, bd0))
+        bg1_early, bu1_early = (lax.ppermute(b[:, :early * BLOCK], 'data', to_core) for b in (bg0, bu0))
         ag, au, ad = (jnp.transpose(a, (0, 2, 1)).reshape(adapters * rank, a.shape[1]) for a in (a_gate, a_up, a_down))
 
         owner = adapter_id // per_owner
@@ -177,27 +221,38 @@
         token = jnp.arange(tok, dtype=jnp.int32)
         before = token[None, :] < token[:, None]
 
-        def place(chosen):
+        def place(chosen, hidden):
             rank_of = jnp.sum((before & chosen[None, :]).astype(jnp.int32), axis=1)
             hot = (token[:, None] == rank_of[None, :]) & chosen[None, :]
             rows = jnp.dot(hot.astype(BF16), hidden, preferred_element_type=F32).astype(BF16)
             lids = jnp.sum(hot.astype(jnp.int32) * (lid[None, :] + 1), axis=1) - 1
             return hot.astype(BF16), rows, lids
 
-        cross_hot, send_x, send_lid = place(cross)
+        cross_hot, send_x, send_lid = place(cross, hidden)
+        send_x, rows = lax.optimization_barrier((send_x, hidden))
         recv_x = lax.ppermute(send_x, 'data', to_chip)
         recv_lid = lax.ppermute(send_lid, 'data', to_chip)
-        stay_hot, stay_x, stay_lid = place(~cross)
-
-        def out_rows(x, lids):
+        stay_hot, stay_x, stay_lid = place(~cross, rows)
+
+        def low(x, lids):
             info = jnp.stack([jnp.sum((lids >= 0).astype(jnp.int32)), me])
             lid_rows = lids[:, None]
             lg, lu = low_rows(info, x, lid_rows, ag, au, own_rows, rank)
-            return mlp(info, x, lid_rows, lg, lu, w_gate, w_up, bg0, bg1, bu0, bu1, w_down, ad, bd0, bd1, rank)
-
-        recv_y = out_rows(recv_x, recv_lid)
+            return info, x, lid_rows, lg, lu, w_gate, w_up
+
+        stay = low(stay_x, stay_lid)
+        late = lax.optimization_barrier((bg0, bu0, bd0, bg1_early, bu1_early, stay))
+        bg1, bu1, bd1 = (lax.ppermute(b, 'data', to_core) for b in late[:3])
+        bg1_early, bu1_early, stay = late[3:]
+        b_all = [(bg0, False), (bg1, False), (bu0, False), (bu1, False)]
+        b_early = [(bg0, False), (bg1_early, True), (bu0, False), (bu1_early, True)]
+        b_out = [bd0, bd1]
+        sums = mlp(*stay, b_early, w_down, ad, None, rank, 0, early)
+        recv_x, recv_lid, sums = lax.optimization_barrier((recv_x, recv_lid, sums))
+        recv_y = mlp(*low(recv_x, recv_lid), b_all, w_down, ad, b_out, rank, 0, blocks)
         back_y = lax.ppermute(recv_y, 'data', to_chip)
-        stay_y = out_rows(stay_x, stay_lid)
+        recv_y, sums = lax.optimization_barrier((recv_y, sums))
+        stay_y = mlp(*stay, b_all, w_down, ad, b_out, rank, early, blocks, sums)
 
         pick = (((0,), (0,)), ((), ()))
         out = lax.dot_general(stay_hot, stay_y, pick, preferred_element_type=F32)

time: 628 us -> 561 us (0.89)
  waiting for transfers between devices: 58.4 us -> 0.02 us
  Pallas kernels: 534 us -> 508 us
  local copies, waits for them, and re-layouts: 1.74 us -> 15.7 us
    ppermute x1, waiting for transfers between devices: 58.4 us -> 0.01 us  [device_fn(): recv_lid = lax.ppermute(send_lid, 'data', to_chip)]
    pallas_call x2 -> x3, Pallas kernels: 510 us -> 484 us  [mlp(): pl.pallas_call(functools.partial(mlp_kernel, counts, rank, sub, wide, res...]
    slice x0 -> x2, local copies, waits for them, and re-layouts: none -> 12.4 us  [device_fn(): b[:, :early * BLOCK]]
  transfers between devices with their start and end apart: 6 -> 8, of which waited for: 1 -> 0; matrix products, arithmetic and copies ran while one was open for 3% -> 5% of each run, Pallas kernels for 46% -> 49%
where the time goes in v1:
time: 561 us; the launch traced here: 554 us
  Pallas kernels  508 us (91%)
  matrix products  18.2 us (3%)
  local copies, waits for them, and re-layouts  15.7 us (3%)
  starting transfers between devices  6.29 us (1%)
  other arithmetic  5.99 us (1%)
    pallas_call x3, Pallas kernels, mlp(): pl.pallas_call(functools.partial(mlp_kernel, counts, rank, sub, wide, res...  484 us
    pallas_call x2, Pallas kernels, low_rows(): pl.pallas_call(functools.partial(low_kernel, counts, rank), grid_spec=plt...  23.4 us
    slice x2, local copies, waits for them, and re-layouts, device_fn(): b[:, :early * BLOCK]  12.4 us
  transfers between devices with their start and end apart: 8, of which 0 were waited for; matrix products, arithmetic and copies ran while one was open for 5% of the time, Pallas kernels for 49%

profile of v1, /device:TPU:0, one launch (start us, length us, event | category | flops | bytes accessed | tf_op | source)
XLA Modules:
  0.0 554.3 jit_solution(10239700204993328238)
XLA Ops:
  0.0 6.2 %slice.9 = bf16[512,6144]{1,0:T(8,128)(2,1)} slice(bf16[512,18944]{1,0:T(8,128)(2,1)} %bitcast.30), slice={[0:512], [0:6144]} | slice | bytes 12582912 | tf_op jit(solution)/shard_map/slice | solution.py:215
  6.2 0.7 collective-permute-start.1
  6.9 0.0 copy-start.9
  6.9 6.2 %slice.8 = bf16[512,6144]{1,0:T(8,128)(2,1)} slice(bf16[512,18944]{1,0:T(8,128)(2,1)} %bitcast.25), slice={[0:512], [0:6144]} | slice | bytes 12582912 | tf_op jit(solution)/shard_map/slice | solution.py:215
  13.1 0.0 collective-permute-start
  13.1 0.0 copy-done.9
  13.1 0.0 copy-start.7
  13.1 0.0 copy-start.5
  13.1 0.1 convert_reduce_fusion.1
  13.3 0.0 copy-start.1
  13.3 0.1 convert_reduce_fusion
  13.4 0.0 copy-start.3
  13.5 0.5 select_reduce_fusion.1
  14.0 0.7 broadcast_add_fusion.1
  14.7 0.8 copy.17.lid_ref
  15.5 0.0 copy-start.10
  15.5 6.1 %convolution_convert_fusion.1 = bf16[512,3584]{1,0:T(8,128)(2,1)} fusion(bf16[512,3584]{1,0:T(8,128)(2,1)} %param.11, s32[512]{0:T(512)S(1)} %convert_reduce_fusion, pred[512]{0:T(512)(128)(4,1)S(1)} %get-tuple-element.60), kind=kOutput, calls=%fused_computation.2 | convolution fusion | flops 1881407488 | bytes 7342592 | tf_op jit(solution)/shard_map/dot_general | solution.py:227
  21.6 0.0 copy-done.7
  21.6 0.0 copy-done.3
  21.6 1.2 pad_add_fusion.info_ref
  22.9 0.0 copy-done.5
  22.9 0.0 copy-done.1
  22.9 0.0 copy-done.10
  22.9 3.8 convolution_convert_fusion.x_ref
  26.7 11.7 %shard_map.109 = (bf16[512,1024]{1,0:T(8,128)(2,1)}, bf16[512,1024]{1,0:T(8,128)(2,1)}) custom-call(s32[2]{0:T(128)} %pad_add_fusion.info_ref, bf16[512,3584]{1,0:T(8,128)(2,1)} %convolution_convert_fusion.x_ref, s32[512,1]{1,0:T(8,128)} %copy.17.lid_ref, bf16[2048,3584]{1,0:T(8,128)(2,1)} %bitcast.21, bf16[2048,3584]{1,0:T(8,128)(2,1)} %bitcast.23), custom_call_target="tpu_custom_call" | custom-call | flops 7516192768 | bytes 14680064 | tf_op jit(solution)/shard_map/pallas_call | solution.py:58
  38.4 0.0 collective-permute-done.1.bu1_ref
  38.4 0.0 collective-permute-done.bg1_ref
  38.4 0.5 collective-permute-start.2
  39.0 0.1 collective-permute-start.3
  39.0 2.9 collective-permute-start.5
  41.9 0.0 collective-permute-start.4
  41.9 0.6 broadcast_add_fusion
  42.5 0.1 collective-permute-start.6
  42.6 0.9 copy.21.lid_ref
  43.5 81.8 %shard_map.110 = (f32[512,3584]{1,0:T(8,128)}, f32[512,1024]{1,0:T(8,128)}) custom-call(s32[2]{0:T(128)} %pad_add_fusion.info_ref, bf16[512,3584]{1,0:T(8,128)(2,1)} %convolution_convert_fusion.x_ref, s32[512,1]{1,0:T(8,128)} %copy.21.lid_ref, bf16[512,1024]{1,0:T(8,128)(2,1)} %get-tuple-element.37.lg_ref, bf16[512,1024]{1,0:T(8,128)(2,1)} %get-tuple-element.38.lu_ref, ...), custom_call_target="tpu_custom_call" | custom-call | flops 1000 | bytes 169869312 | tf_op jit(solution)/shard_map/pallas_call | solution.py:178
  125.3 0.0 collective-permute-done.6
  125.3 0.0 collective-permute-done.5.x_ref
  125.3 1.5 copy.20.lid_ref
  126.9 1.3 convert_reduce_fusion.2
  128.2 1.3 pad_add_fusion.1.info_ref
  129.5 11.7 %shard_map.111 = (bf16[512,1024]{1,0:T(8,128)(2,1)}, bf16[512,1024]{1,0:T(8,128)(2,1)}) custom-call(s32[2]{0:T(128)} %pad_add_fusion.1.info_ref, bf16[512,3584]{1,0:T(8,128)(2,1)} %collective-permute-done.5.x_ref, s32[512,1]{1,0:T(8,128)} %copy.20.lid_ref, bf16[2048,3584]{1,0:T(8,128)(2,1)} %bitcast.22, bf16[2048,3584]{1,0:T(8,128)(2,1)} %bitcast.24), custom_call_target="tpu_custom_call" | custom-call | flops 7516192768 | bytes 14680064 | tf_op jit(solution)/shard_map/pallas_call | solution.py:58
  141.2 0.0 collective-permute-done.4.refs_1_
  141.2 0.0 collective-permute-done.2.bg1_ref
  141.2 0.0 collective-permute-done.3.bu1_ref
  141.2 238.7 %shard_map.112 = bf16[512,3584]{1,0:T(8,128)(2,1)} custom-call(s32[2]{0:T(128)} %pad_add_fusion.1.info_ref, bf16[512,3584]{1,0:T(8,128)(2,1)} %collective-permute-done.5.x_ref, s32[512,1]{1,0:T(8,128)} %copy.20.lid_ref, bf16[512,1024]{1,0:T(8,128)(2,1)} %get-tuple-element.51.lg_ref, bf16[512,1024]{1,0:T(8,128)(2,1)} %get-tuple-element.52.lu_ref, ...), custom_call_target="tpu_custom_call" | custom-call | flops 268167020544 | bytes 523763712 | tf_op jit(solution)/shard_map/pallas_call | solution.py:178
  379.9 2.0 collective-permute-start.7
  381.9 0.0 copy-start.4
  381.9 0.0 copy-start.8
  381.9 163.8 %shard_map.113 = bf16[512,3584]{1,0:T(8,128)(2,1)} custom-call(s32[2]{0:T(128)} %pad_add_fusion.info_ref, bf16[512,3584]{1,0:T(8,128)(2,1)} %convolution_convert_fusion.x_ref, s32[512,1]{1,0:T(8,128)} %copy.21.lid_ref, bf16[512,1024]{1,0:T(8,128)(2,1)} %get-tuple-element.37.lg_ref, bf16[512,1024]{1,0:T(8,128)(2,1)} %get-tuple-element.38.lu_ref, ...), custom_call_target="tpu_custom_call" | custom-call | flops 181193932800 | bytes 353894400 | tf_op jit(solution)/shard_map/pallas_call | solution.py:178
  545.7 0.0 copy-start
  545.7 0.0 copy-start.2
  545.7 0.0 copy-start.6
  545.7 0.0 collective-permute-done.7
  545.7 0.0 copy-done.4
  545.8 0.0 copy-done.8
  545.8 4.3 fusion.6
  550.1 0.0 copy-done
  550.1 0.0 copy-done.2
  550.1 0.0 copy-done.6
  550.1 4.0 add_convert_fusion
  (2 shorter events, 0.0 us)
Async XLA Ops:
  6.2 32.2 %collective-permute-start.1 = (bf16[512,6144]{1,0:T(8,128)(2,1)}, bf16[512,6144]{1,0:T(8,128)(2,1)}, u32[]{:S(2)}, u32[]{:S(2)}) collective-permute-start(bf16[512,6144]{1,0:T(8,128)(2,1)} %slice.9), channel_id=1, source_target_pairs={{0,1},{1,0},{2,3},{3,2},{4,5},{5,4},{6,7},{7,6},{8,9},{9,8},{10,11... | collective-permute-start | bytes 18874376 | tf_op jit(solution)/shard_map/ppermute | solution.py:215
  6.9 6.2 %copy-start.9 = (s32[512]{0:T(512)S(1)}, s32[512]{0:T(512)}, u32[]{:S(2)}) copy-start(s32[512]{0:T(512)} %param.12) | copy-start | bytes 6148
  13.1 25.3 %collective-permute-start = (bf16[512,6144]{1,0:T(8,128)(2,1)}, bf16[512,6144]{1,0:T(8,128)(2,1)}, u32[]{:S(2)}, u32[]{:S(2)}) collective-permute-start(bf16[512,6144]{1,0:T(8,128)(2,1)} %slice.8), channel_id=1, source_target_pairs={{0,1},{1,0},{2,3},{3,2},{4,5},{5,4},{6,7},{7,6},{8,9},{9,8},{10,11... | collective-permute-start | bytes 18874376 | tf_op jit(solution)/shard_map/ppermute | solution.py:215
  13.1 8.5 %copy-start.7 = (pred[512]{0:T(512)(128)(4,1)}, pred[512]{0:T(512)(128)(4,1)S(1)}, u32[]{:S(2)}) copy-start(pred[512]{0:T(512)(128)(4,1)S(1)} %get-tuple-element.60) | copy-start | bytes 1540
  13.1 9.8 %copy-start.5 = (pred[512]{0:T(512)(128)(4,1)}, pred[512]{0:T(512)(128)(4,1)S(1)}, u32[]{:S(2)}) copy-start(pred[512]{0:T(512)(128)(4,1)S(1)} %get-tuple-element.59) | copy-start | bytes 1540
  13.3 9.6 %copy-start.1 = (s32[512]{0:T(512)}, s32[512]{0:T(512)S(1)}, u32[]{:S(2)}) copy-start(s32[512]{0:T(512)S(1)} %convert_reduce_fusion.1) | copy-start | bytes 6148
  13.4 8.2 %copy-start.3 = (s32[512]{0:T(512)}, s32[512]{0:T(512)S(1)}, u32[]{:S(2)}) copy-start(s32[512]{0:T(512)S(1)} %convert_reduce_fusion) | copy-start | bytes 6148
  15.5 7.3 %copy-start.10 = (bf16[512,3584]{1,0:T(8,128)(2,1)S(1)}, bf16[512,3584]{1,0:T(8,128)(2,1)}, u32[]{:S(2)}) copy-start(bf16[512,3584]{1,0:T(8,128)(2,1)} %param.11) | copy-start | bytes 11010052
  38.4 102.8 %collective-permute-start.2 = (bf16[512,18944]{1,0:T(8,128)(2,1)}, bf16[512,18944]{1,0:T(8,128)(2,1)}, u32[]{:S(2)}, u32[]{:S(2)}) collective-permute-start(bf16[512,18944]{1,0:T(8,128)(2,1)} %bitcast.26), channel_id=1, source_target_pairs={{0,1},{1,0},{2,3},{3,2},{4,5},{5,4},{6,7},{7,6},{8,9},{9,8},{10,11... | collective-permute-start | bytes 58195976 | tf_op jit(solution)/shard_map/ppermute | solution.py:245
  39.0 102.2 %collective-permute-start.3 = (bf16[512,18944]{1,0:T(8,128)(2,1)}, bf16[512,18944]{1,0:T(8,128)(2,1)}, u32[]{:S(2)}, u32[]{:S(2)}) collective-permute-start(bf16[512,18944]{1,0:T(8,128)(2,1)} %bitcast.31), channel_id=1, source_target_pairs={{0,1},{1,0},{2,3},{3,2},{4,5},{5,4},{6,7},{7,6},{8,9},{9,8},{10,11... | collective-permute-start | bytes 58195976 | tf_op jit(solution)/shard_map/ppermute | solution.py:245
  39.0 86.3 %collective-permute-start.5 = (bf16[512,3584]{1,0:T(8,128)(2,1)}, bf16[512,3584]{1,0:T(8,128)(2,1)}, u32[]{:S(2)}, u32[]{:S(2)}) collective-permute-start(bf16[512,3584]{1,0:T(8,128)(2,1)} %convolution_convert_fusion.1), channel_id=1, source_target_pairs={{0,2},{1,3},{2,0},{3,1},{4,6},{5,7},{6,4},{7,5},{8,10},{9,11},{10,... | collective-permute-start | bytes 11010056 | tf_op jit(solution)/shard_map/ppermute | solution.py:233
  41.9 99.2 %collective-permute-start.4 = (bf16[512,3584]{1,0:T(8,128)(2,1)}, bf16[512,3584]{1,0:T(8,128)(2,1)}, u32[]{:S(2)}, u32[]{:S(2)}) collective-permute-start(bf16[512,3584]{1,0:T(8,128)(2,1)} %bitcast.37), channel_id=1, source_target_pairs={{0,1},{1,0},{2,3},{3,2},{4,5},{5,4},{6,7},{7,6},{8,9},{9,8},{10,11... | collective-permute-start | bytes 11010056 | tf_op jit(solution)/shard_map/ppermute | solution.py:245
  42.5 82.8 %collective-permute-start.6 = (s32[512]{0:T(512)}, s32[512]{0:T(512)}, u32[]{:S(2)}, u32[]{:S(2)}) collective-permute-start(s32[512]{0:T(512)} %broadcast_add_fusion), channel_id=1, source_target_pairs={{0,2},{1,3},{2,0},{3,1},{4,6},{5,7},{6,4},{7,5},{8,10},{9,11},{10,... | collective-permute-start | bytes 6152 | tf_op jit(solution)/shard_map/ppermute | solution.py:234
  379.9 165.8 %collective-permute-start.7 = (bf16[512,3584]{1,0:T(8,128)(2,1)}, bf16[512,3584]{1,0:T(8,128)(2,1)}, u32[]{:S(2)}, u32[]{:S(2)}) collective-permute-start(bf16[512,3584]{1,0:T(8,128)(2,1)} %shard_map.112), channel_id=1, source_target_pairs={{0,2},{1,3},{2,0},{3,1},{4,6},{5,7},{6,4},{7,5},{8,10},{9,11},{10,... | collective-permute-start | bytes 11010056 | tf_op jit(solution)/shard_map/ppermute | solution.py:253
  381.9 163.9 %copy-start.4 = (s32[512]{0:T(512)S(1)}, s32[512]{0:T(512)}, u32[]{:S(2)}) copy-start(s32[512]{0:T(512)} %copy-done.3) | copy-start | bytes 6148
  381.9 163.9 %copy-start.8 = (pred[512]{0:T(512)(128)(4,1)S(1)}, pred[512]{0:T(512)(128)(4,1)}, u32[]{:S(2)}) copy-start(pred[512]{0:T(512)(128)(4,1)} %copy-done.7) | copy-start | bytes 1540
  545.7 4.4 copy-start
  545.7 4.4 copy-start.2
  545.7 4.4 copy-start.6

commit v2 on v1

--- a/solution.py
+++ b/solution.py
@@ -16,18 +16,15 @@
 BLOCK = 512
 
 
-def row_counts(tok):
+def row_cases(tok):
     if tok == 512:
-        return (352, 368, 512)
-    return (tok // 2, tok)
-
-
-def per_row_count(rows_ref, counts, body):
-    rows = rows_ref[0]
-    below = 0
-    for count in counts:
-        pl.when((rows > below) & (rows <= count))(functools.partial(body, count))
-        below = count
+        return ((256, 352), (96, 352), (256, 368), (112, 368), (256, 512))
+    return ((tok // 2, tok),)
+
+
+def per_case(info_ref, tok, body):
+    for index, (split, rows) in enumerate(row_cases(tok)):
+        pl.when(info_ref[0] == index)(functools.partial(body, split, rows))
 
 
 def whole(shape):
@@ -35,41 +32,43 @@
     return pl.BlockSpec(shape, lambda *_: zeros, pipeline_mode=pl.Buffered(1))
 
 
-def low_kernel(counts, rank, info_ref, x_ref, lid_ref, ag_ref, au_ref, lg_ref, lu_ref):
-    width = ag_ref.shape[0]
+def low_kernel(rank, info_ref, x_ref, lid_ref, ag0_ref, ag1_ref, au0_ref, au1_ref, lg_ref, lu_ref):
+    width = ag0_ref.shape[0]
     block = pl.program_id(0)
 
-    def body(m):
-        column = block * width + lax.broadcasted_iota(jnp.int32, (m, width), 1)
-        mine = (column // rank) == lid_ref[:m, :]
-        for a_ref, l_ref in ((ag_ref, lg_ref), (au_ref, lu_ref)):
-            low = lax.dot_general(x_ref[:m, :], a_ref[...], NT, preferred_element_type=F32)
-            l_ref[:m, :] = jnp.where(mine, low, 0.0).astype(BF16)
-
-    per_row_count(info_ref, counts, body)
+    def body(split, m):
+        def masked(rows, a_ref):
+            low = lax.dot_general(x_ref[rows, :], a_ref[...], NT, preferred_element_type=F32)
+            column = block * width + lax.broadcasted_iota(jnp.int32, low.shape, 1)
+            return jnp.where((column // rank) == lid_ref[rows, :], low, 0.0).astype(BF16)
+
+        for a0_ref, a1_ref, l_ref in ((ag0_ref, ag1_ref, lg_ref), (au0_ref, au1_ref, lu_ref)):
+            l_ref[:split, :] = masked(slice(0, split), a0_ref)
+            l_ref[split:m, :] = masked(slice(split, m), a1_ref)
+
+    per_case(info_ref, x_ref.shape[0], body)
 
 
 def low_rows(info, x, lid, ag, au, own_rows, rank):
     tok, d = x.shape
     width = own_rows // 2
-    counts = row_counts(tok)
-    spec_a = pl.BlockSpec((width, d), lambda b, info: ((info[1] ^ (b // 2)) * 2 + b % 2, 0))
+    spec_a = [pl.BlockSpec((width, d), lambda b, info, side=side: ((info[1] ^ side) * 2 + b, 0)) for side in (0, 1)]
     spec_l = pl.BlockSpec((tok, width), lambda b, info: (0, b))
     return pl.pallas_call(
-        functools.partial(low_kernel, counts, rank),
+        functools.partial(low_kernel, rank),
         grid_spec=pltpu.PrefetchScalarGridSpec(
             num_scalar_prefetch=1,
-            grid=(4,),
-            in_specs=[whole((tok, d)), whole((tok, 1)), spec_a, spec_a],
+            grid=(2,),
+            in_specs=[whole((tok, d)), whole((tok, 1)), *spec_a, *spec_a],
             out_specs=[spec_l, spec_l],
         ),
-        out_shape=[jax.ShapeDtypeStruct((tok, 4 * width), BF16)] * 2,
+        out_shape=[jax.ShapeDtypeStruct((tok, own_rows), BF16)] * 2,
         compiler_params=pltpu.CompilerParams(vmem_limit_bytes=VMEM_LIMIT),
-        cost_estimate=pl.CostEstimate(flops=2 * 2 * tok * d * 4 * width, bytes_accessed=4 * 4 * width * d, transcendentals=0),
-    )(info, x, lid, ag, au)
-
-
-def mlp_kernel(counts, rank, sub, wide, resume, final, info_ref, x_ref, lid_ref, lg_ref, lu_ref, wg_ref, wu_ref, bg0_ref, bg1_ref,
+        cost_estimate=pl.CostEstimate(flops=4 * tok * d * own_rows, bytes_accessed=8 * own_rows * d, transcendentals=0),
+    )(info, x, lid, ag, ag, au, au)
+
+
+def mlp_kernel(rank, sub, wide, resume, final, info_ref, x_ref, lid_ref, lg_ref, lu_ref, wg_ref, wu_ref, bg0_ref, bg1_ref,
                bu0_ref, bu1_ref, wd_ref, a0_ref, a1_ref, *refs):
     refs = list(refs)
     bd0_ref, bd1_ref = (refs.pop(0), refs.pop(0)) if final else (None, None)
@@ -89,12 +88,15 @@
         for copy in copies:
             copy.wait()
 
-    def body(m):
+    def body(split, m):
+        def spread(l_ref, at, b0_ref, b1_ref):
+            own = jnp.dot(l_ref[:split, :], b0_ref[:, at], preferred_element_type=F32)
+            partner = jnp.dot(l_ref[split:m, :], b1_ref[:, at], preferred_element_type=F32)
+            return (LORA_SCALE * jnp.concatenate([own, partner], axis=0)).astype(BF16).astype(F32)
+
         def branch(at, w_ref, l_ref, b0_ref, b1_ref):
             base = jnp.dot(x_ref[:m, :], w_ref[:, at], preferred_element_type=F32)
-            delta = jnp.dot(l_ref[:m, :half], b0_ref[:, at], preferred_element_type=F32)
-            delta += jnp.dot(l_ref[:m, half:], b1_ref[:, at], preferred_element_type=F32)
-            return base + (LORA_SCALE * delta).astype(BF16).astype(F32)
+            return base + spread(l_ref, at, b0_ref, b1_ref)
 
         @pl.when(step == 0)
         def _():
@@ -102,19 +104,18 @@
                 move(((acc_in, acc_ref), (low_in, low_ref)))
             else:
                 acc_ref[:m, :] = jnp.zeros((m, d), F32)
-                low_ref[:m, :] = jnp.zeros((m, 2 * half), F32)
+                low_ref[:m, :] = jnp.zeros((m, half), F32)
 
         def gate_up(at):
             return at, branch(at, wg_ref, lg_ref, bg0_ref, bg1_ref), branch(at, wu_ref, lu_ref, bu0_ref, bu1_ref)
 
         def add_down(at, gate, up):
             h = (jax.nn.silu(gate) * up).astype(BF16)
+            for rows, a_ref in ((slice(0, split), a0_ref), (slice(split, m), a1_ref)):
+                low_ref[rows, :] += lax.dot_general(h[rows, :], a_ref[:, at], NT, preferred_element_type=F32)
             for left in range(0, d, wide):
                 to = slice(left, left + wide)
                 acc_ref[:m, to] += jnp.dot(h, wd_ref[at, to], preferred_element_type=F32)
-            for side, a_ref in ((0, a0_ref), (1, a1_ref)):
-                to = slice(side * half, (side + 1) * half)
-                low_ref[:m, to] += lax.dot_general(h, a_ref[:, at], NT, preferred_element_type=F32)
 
         waiting = None
         for first in range(0, block, sub):
@@ -129,15 +130,13 @@
             if not final:
                 move(((acc_ref, acc_out), (low_ref, low_out)))
                 return
-            column = lax.broadcasted_iota(jnp.int32, (m, 2 * half), 1)
+            column = lax.broadcasted_iota(jnp.int32, (m, half), 1)
             mine = (column // rank) == lid_ref[:m, :]
             ld_ref[:m, :] = jnp.where(mine, low_ref[:m, :], 0.0).astype(BF16)
 
             def finish(i, carry):
                 to = pl.ds(pl.multiple_of(i * wide, wide), wide)
-                delta = jnp.dot(ld_ref[:m, :half], bd0_ref[:, to], preferred_element_type=F32)
-                delta += jnp.dot(ld_ref[:m, half:], bd1_ref[:, to], preferred_element_type=F32)
-                down = acc_ref[:m, to] + (LORA_SCALE * delta).astype(BF16).astype(F32)
+                down = acc_ref[:m, to] + spread(ld_ref, to, bd0_ref, bd1_ref)
                 o_ref[:m, to] = (x_ref[:m, to].astype(F32) + down).astype(BF16)
                 return carry
 
@@ -145,14 +144,12 @@
             if m < tok:
                 o_ref[m:, :] = jnp.zeros((tok - m, d), BF16)
 
-    per_row_count(info_ref, counts, body)
+    per_case(info_ref, tok, body)
 
 
 def mlp(info, x, lid, lg, lu, wg, wu, bs, wd, ad, bd, rank, first, stop, sums=None, block=BLOCK, sub=256, wide=512):
     tok, d = x.shape
-    low = lg.shape[1]
-    half = low // 2
-    counts = row_counts(tok)
+    low = half = lg.shape[1]
     resume, final = sums is not None, bd is not None
     spec_w = pl.BlockSpec((d, block), lambda i, info: (0, i + first))
     any_spec = pl.BlockSpec(memory_space=pl.ANY)
@@ -176,7 +173,7 @@
         args += sums
     width = (stop - first) * block
     return pl.pallas_call(
-        functools.partial(mlp_kernel, counts, rank, sub, wide, resume, final),
+        functools.partial(mlp_kernel, rank, sub, wide, resume, final),
         grid_spec=pltpu.PrefetchScalarGridSpec(
             num_scalar_prefetch=1,
             grid=(stop - first,),
@@ -209,34 +206,41 @@
         me = lax.axis_index('data').astype(jnp.int32)
 
         blocks = f // BLOCK
-        early = max(1, blocks // 3)
+        early = max(1, blocks // 4)
 
         bg0, bu0, bd0 = (b.reshape(own_rows, b.shape[2]) for b in (b_gate, b_up, b_down))
-        bg1_early, bu1_early = (lax.ppermute(b[:, :early * BLOCK], 'data', to_core) for b in (bg0, bu0))
         ag, au, ad = (jnp.transpose(a, (0, 2, 1)).reshape(adapters * rank, a.shape[1]) for a in (a_gate, a_up, a_down))
 
         owner = adapter_id // per_owner
         cross = (owner // 2) != (me // 2)
-        lid = ((owner ^ me) & 1) * per_owner + adapter_id % per_owner
+        partner = ((owner ^ me) & 1) == 1
+        lid = adapter_id % per_owner
         token = jnp.arange(tok, dtype=jnp.int32)
         before = token[None, :] < token[:, None]
+        splits, sizes = (jnp.array(column, jnp.int32) for column in zip(*row_cases(tok)))
 
         def place(chosen, hidden):
-            rank_of = jnp.sum((before & chosen[None, :]).astype(jnp.int32), axis=1)
+            own = jnp.sum((chosen & ~partner).astype(jnp.int32))
+            other = jnp.sum((chosen & partner).astype(jnp.int32))
+            case = jnp.argmax((own <= splits) & (other <= sizes - splits)).astype(jnp.int32)
+            alike = before & chosen[None, :] & (partner[None, :] == partner[:, None])
+            rank_of = jnp.sum(alike.astype(jnp.int32), axis=1) + jnp.where(partner, splits[case], 0)
             hot = (token[:, None] == rank_of[None, :]) & chosen[None, :]
             rows = jnp.dot(hot.astype(BF16), hidden, preferred_element_type=F32).astype(BF16)
             lids = jnp.sum(hot.astype(jnp.int32) * (lid[None, :] + 1), axis=1) - 1
-            return hot.astype(BF16), rows, lids
+            return hot.astype(BF16), rows, jnp.concatenate([lids, jnp.full((128,), case, jnp.int32)])
 
         cross_hot, send_x, send_lid = place(cross, hidden)
-        send_x, rows = lax.optimization_barrier((send_x, hidden))
+        send_x, rows, bg0_cut, bu0_cut = lax.optimization_barrier((send_x, hidden, bg0, bu0))
         recv_x = lax.ppermute(send_x, 'data', to_chip)
         recv_lid = lax.ppermute(send_lid, 'data', to_chip)
+        cuts = [b[:, :early * BLOCK] for b in (bg0_cut, bu0_cut)]
+        bg1_early, bu1_early = (lax.ppermute(b, 'data', to_core) for b in cuts)
         stay_hot, stay_x, stay_lid = place(~cross, rows)
 
         def low(x, lids):
-            info = jnp.stack([jnp.sum((lids >= 0).astype(jnp.int32)), me])
-            lid_rows = lids[:, None]
+            info = jnp.stack([lids[tok], me])
+            lid_rows = lids[:tok, None]
             lg, lu = low_rows(info, x, lid_rows, ag, au, own_rows, rank)
             return info, x, lid_rows, lg, lu, w_gate, w_up
 

time: 561 us -> 546 us (0.973)
  Pallas kernels: 508 us -> 474 us
    pallas_call x5, Pallas kernels: 508 us -> 474 us  [the longest x3 452 us: mlp(): pl.pallas_call(functools.partial(mlp_kernel, rank, sub, wide, resume, fin...]
    slice x2 -> x4, local copies, waits for them, and re-layouts: 12.4 us -> 11.4 us  [the longest x2 9.57 us: device_fn(): cuts = [b[:, :early * BLOCK] for b in (bg0_cut, bu0_cut)]]
  transfers between devices with their start and end apart: 8 -> 8, of which waited for: 0 -> 1; matrix products, arithmetic and copies ran while one was open for 5% -> 4% of each run, Pallas kernels for 49% -> 48%
where the time goes in v2:
time: 546 us; the launch traced here: 537 us
  Pallas kernels  474 us (87%)
  matrix products  20.2 us (4%)
  local copies, waits for them, and re-layouts  17.8 us (3%)
  other arithmetic  10.2 us (2%)
  starting transfers between devices  6.25 us (1%)
    pallas_call x3, Pallas kernels, mlp(): pl.pallas_call(functools.partial(mlp_kernel, rank, sub, wide, resume, fin...  452 us
    pallas_call x2, Pallas kernels, low_rows(): pl.pallas_call(functools.partial(low_kernel, rank), grid_spec=pltpu.Prefe...  21.5 us
    dot_general x2, matrix products, place(): jnp.dot(hot.astype(BF16), hidden, preferred_element_type=F32).astype(BF16)  11.9 us
  transfers between devices with their start and end apart: 8, of which 1 were waited for; matrix products, arithmetic and copies ran while one was open for 4% of the time, Pallas kernels for 48%

profile of v2, /device:TPU:0, one launch (start us, length us, event | category | flops | bytes accessed | tf_op | source)
XLA Modules:
  0.0 536.8 jit_solution(272102619278742649)
XLA Ops:
  0.0 0.7 fusion.19
  0.7 0.7 convert_reduce_fusion.5
  1.4 0.0 copy-start.5
  1.4 2.7 and_reduce_fusion.1
  5.3 2.6 and_reduce_fusion
  9.1 0.0 copy-start.7
  10.3 1.3 fusion.23
  11.7 0.4 convert_reduce_fusion.1
  12.1 1.3 select_add_fusion.1
  13.4 0.0 copy-start.3
  13.4 0.0 copy-start.1
  13.4 5.9 %convolution_convert_fusion.1 = bf16[512,3584]{1,0:T(8,128)(2,1)} fusion(bf16[512,3584]{1,0:T(8,128)(2,1)} %param.13, s32[512]{0:T(512)S(1)} %get-tuple-element.78, pred[512]{0:T(512)(128)(4,1)S(1)} %get-tuple-element.73), kind=kOutput, calls=%fused_computation.2 | convolution fusion | flops 1881407488 | bytes 7342592 | tf_op jit(solution)/shard_map/dot_general | solution.py:229
  19.3 4.8 slice.14
  24.1 0.7 collective-permute-start.1
  24.8 4.8 slice.13
  29.6 0.0 collective-permute-start
  29.6 1.2 stack.11.info_ref
  30.8 0.0 copy-done.5
  30.8 0.0 copy-done.3
  30.8 0.5 select_reduce_fusion.1
  31.4 0.9 copy.19.lid_ref
  32.2 0.0 copy-done.7
  32.2 0.0 copy-done.1
  32.2 5.9 %convolution_convert_fusion.x_ref = bf16[512,3584]{1,0:T(8,128)(2,1)} fusion(bf16[512,3584]{1,0:T(8,128)(2,1)} %param.13, s32[512]{0:T(512)S(1)} %get-tuple-element.77, pred[512]{0:T(512)(128)(4,1)S(1)} %not.7), kind=kOutput, calls=%fused_computation.1 | convolution fusion | flops 1881407488 | bytes 7342592 | tf_op jit(solution)/shard_map/dot_general | solution.py:229
  38.2 10.7 %shard_map.127 = (bf16[512,512]{1,0:T(8,128)(2,1)}, bf16[512,512]{1,0:T(8,128)(2,1)}) custom-call(s32[2]{0:T(128)} %stack.11.info_ref, bf16[512,3584]{1,0:T(8,128)(2,1)} %convolution_convert_fusion.x_ref, s32[512,1]{1,0:T(8,128)} %copy.19.lid_ref, bf16[2048,3584]{1,0:T(8,128)(2,1)} %bitcast.21, bf16[2048,3584]{1,0:T(8,128)(2,1)} %bitcast.22, ...), custom_call_target="tpu_custom_call" | custom-call | flops 3758096384 | bytes 14680064 | tf_op jit(solution)/shard_map/pallas_call | solution.py:57
  48.9 0.0 collective-permute-done.1.bu1_ref
  48.9 0.0 collective-permute-done.bg1_ref
  48.9 0.5 collective-permute-start.2
  49.5 0.1 collective-permute-start.3
  49.5 2.9 collective-permute-start.5
  52.5 0.0 collective-permute-start.4
  52.5 1.2 concatenate.3
  53.6 0.1 collective-permute-start.6
  53.7 0.9 copy.23.lid_ref
  54.5 73.6 %shard_map.128 = (f32[512,3584]{1,0:T(8,128)}, f32[512,512]{1,0:T(8,128)}) custom-call(s32[2]{0:T(128)} %stack.11.info_ref, bf16[512,3584]{1,0:T(8,128)(2,1)} %convolution_convert_fusion.x_ref, s32[512,1]{1,0:T(8,128)} %copy.23.lid_ref, bf16[512,512]{1,0:T(8,128)(2,1)} %get-tuple-element.45.lg_ref, bf16[512,512]{1,0:T(8,128)(2,1)} %get-tuple-element.46.lu_ref, ...), custom_call_target="tpu_custom_call" | custom-call | flops 1000 | bytes 113246208 | tf_op jit(solution)/shard_map/pallas_call | solution.py:175
  128.1 4.3 collective-permute-done.6
  132.4 0.0 collective-permute-done.5.x_ref
  132.4 1.2 slice.15
  133.6 0.7 slice.16
  134.3 0.9 copy.22.lid_ref
  135.2 1.3 pad_add_fusion.info_ref
  136.5 10.7 %shard_map.129 = (bf16[512,512]{1,0:T(8,128)(2,1)}, bf16[512,512]{1,0:T(8,128)(2,1)}) custom-call(s32[2]{0:T(128)} %pad_add_fusion.info_ref, bf16[512,3584]{1,0:T(8,128)(2,1)} %collective-permute-done.5.x_ref, s32[512,1]{1,0:T(8,128)} %copy.22.lid_ref, bf16[2048,3584]{1,0:T(8,128)(2,1)} %bitcast.23, bf16[2048,3584]{1,0:T(8,128)(2,1)} %bitcast.24, ...), custom_call_target="tpu_custom_call" | custom-call | flops 3758096384 | bytes 14680064 | tf_op jit(solution)/shard_map/pallas_call | solution.py:57
  147.2 0.0 collective-permute-done.4.refs_1_
  147.2 0.0 collective-permute-done.2.bg1_ref
  147.2 0.0 collective-permute-done.3.bu1_ref
  147.2 217.4 %shard_map.130 = bf16[512,3584]{1,0:T(8,128)(2,1)} custom-call(s32[2]{0:T(128)} %pad_add_fusion.info_ref, bf16[512,3584]{1,0:T(8,128)(2,1)} %collective-permute-done.5.x_ref, s32[512,1]{1,0:T(8,128)} %copy.22.lid_ref, bf16[512,512]{1,0:T(8,128)(2,1)} %get-tuple-element.59.lg_ref, bf16[512,512]{1,0:T(8,128)(2,1)} %get-tuple-element.60.lu_ref, ...), custom_call_target="tpu_custom_call" | custom-call | flops 238370684928 | bytes 465567744 | tf_op jit(solution)/shard_map/pallas_call | solution.py:175
  364.7 1.9 collective-permute-start.7
  366.6 0.0 copy-start.4
  366.6 0.0 copy-start.6
  366.6 161.4 %shard_map.131 = bf16[512,3584]{1,0:T(8,128)(2,1)} custom-call(s32[2]{0:T(128)} %stack.11.info_ref, bf16[512,3584]{1,0:T(8,128)(2,1)} %convolution_convert_fusion.x_ref, s32[512,1]{1,0:T(8,128)} %copy.23.lid_ref, bf16[512,512]{1,0:T(8,128)(2,1)} %get-tuple-element.45.lg_ref, bf16[512,512]{1,0:T(8,128)(2,1)} %get-tuple-element.46.lu_ref, ...), custom_call_target="tpu_custom_call" | custom-call | flops 180388626432 | bytes 352321536 | tf_op jit(solution)/shard_map/pallas_call | solution.py:175
  528.0 0.0 copy-start
  528.0 0.0 copy-start.2
  528.0 0.0 copy-start.8
  528.0 0.0 collective-permute-done.7
  528.0 0.0 copy-done.4
  528.1 0.0 copy-done.6
  528.1 4.3 fusion.6
  532.4 0.0 copy-done
  532.4 0.0 copy-done.2
  532.4 0.0 copy-done.8
  532.4 4.0 add_convert_fusion
  (3 shorter events, 0.0 us)
Async XLA Ops:
  1.4 29.4 %copy-start.5 = (pred[512]{0:T(512)(128)(4,1)}, pred[512]{0:T(512)(128)(4,1)S(1)}, u32[]{:S(2)}) copy-start(pred[512]{0:T(512)(128)(4,1)S(1)} %get-tuple-element.73) | copy-start | bytes 1540
  9.1 23.1 %copy-start.7 = (pred[512]{0:T(512)(128)(4,1)}, pred[512]{0:T(512)(128)(4,1)S(1)}, u32[]{:S(2)}) copy-start(pred[512]{0:T(512)(128)(4,1)S(1)} %not.7) | copy-start | bytes 1540
  13.4 17.5 %copy-start.3 = (s32[512]{0:T(512)}, s32[512]{0:T(512)S(1)}, u32[]{:S(2)}) copy-start(s32[512]{0:T(512)S(1)} %get-tuple-element.78) | copy-start | bytes 6148
  13.4 18.9 %copy-start.1 = (s32[512]{0:T(512)}, s32[512]{0:T(512)S(1)}, u32[]{:S(2)}) copy-start(s32[512]{0:T(512)S(1)} %get-tuple-element.77) | copy-start | bytes 6148
  24.1 24.9 %collective-permute-start.1 = (bf16[512,4608]{1,0:T(8,128)(2,1)}, bf16[512,4608]{1,0:T(8,128)(2,1)}, u32[]{:S(2)}, u32[]{:S(2)}) collective-permute-start(bf16[512,4608]{1,0:T(8,128)(2,1)} %slice.14), channel_id=1, source_target_pairs={{0,1},{1,0},{2,3},{3,2},{4,5},{5,4},{6,7},{7,6},{8,9},{9,8},{10,11... | collective-permute-start | bytes 14155784 | tf_op jit(solution)/shard_map/ppermute | solution.py:238
  29.6 19.3 %collective-permute-start = (bf16[512,4608]{1,0:T(8,128)(2,1)}, bf16[512,4608]{1,0:T(8,128)(2,1)}, u32[]{:S(2)}, u32[]{:S(2)}) collective-permute-start(bf16[512,4608]{1,0:T(8,128)(2,1)} %slice.13), channel_id=1, source_target_pairs={{0,1},{1,0},{2,3},{3,2},{4,5},{5,4},{6,7},{7,6},{8,9},{9,8},{10,11... | collective-permute-start | bytes 14155784 | tf_op jit(solution)/shard_map/ppermute | solution.py:238
  48.9 98.3 %collective-permute-start.2 = (bf16[512,18944]{1,0:T(8,128)(2,1)}, bf16[512,18944]{1,0:T(8,128)(2,1)}, u32[]{:S(2)}, u32[]{:S(2)}) collective-permute-start(bf16[512,18944]{1,0:T(8,128)(2,1)} %bitcast.30), channel_id=1, source_target_pairs={{0,1},{1,0},{2,3},{3,2},{4,5},{5,4},{6,7},{7,6},{8,9},{9,8},{10,11... | collective-permute-start | bytes 58195976 | tf_op jit(solution)/shard_map/ppermute | solution.py:249
  49.5 97.7 %collective-permute-start.3 = (bf16[512,18944]{1,0:T(8,128)(2,1)}, bf16[512,18944]{1,0:T(8,128)(2,1)}, u32[]{:S(2)}, u32[]{:S(2)}) collective-permute-start(bf16[512,18944]{1,0:T(8,128)(2,1)} %bitcast.35), channel_id=1, source_target_pairs={{0,1},{1,0},{2,3},{3,2},{4,5},{5,4},{6,7},{7,6},{8,9},{9,8},{10,11... | collective-permute-start | bytes 58195976 | tf_op jit(solution)/shard_map/ppermute | solution.py:249
  49.5 82.9 %collective-permute-start.5 = (bf16[512,3584]{1,0:T(8,128)(2,1)}, bf16[512,3584]{1,0:T(8,128)(2,1)}, u32[]{:S(2)}, u32[]{:S(2)}) collective-permute-start(bf16[512,3584]{1,0:T(8,128)(2,1)} %convolution_convert_fusion.1), channel_id=1, source_target_pairs={{0,2},{1,3},{2,0},{3,1},{4,6},{5,7},{6,4},{7,5},{8,10},{9,11},{10,... | collective-permute-start | bytes 11010056 | tf_op jit(solution)/shard_map/ppermute | solution.py:235
  52.5 94.7 %collective-permute-start.4 = (bf16[512,3584]{1,0:T(8,128)(2,1)}, bf16[512,3584]{1,0:T(8,128)(2,1)}, u32[]{:S(2)}, u32[]{:S(2)}) collective-permute-start(bf16[512,3584]{1,0:T(8,128)(2,1)} %bitcast.42), channel_id=1, source_target_pairs={{0,1},{1,0},{2,3},{3,2},{4,5},{5,4},{6,7},{7,6},{8,9},{9,8},{10,11... | collective-permute-start | bytes 11010056 | tf_op jit(solution)/shard_map/ppermute | solution.py:249
  53.6 78.8 %collective-permute-start.6 = (s32[640]{0:T(1024)}, s32[640]{0:T(1024)}, u32[]{:S(2)}, u32[]{:S(2)}) collective-permute-start(s32[640]{0:T(1024)} %concatenate.3), channel_id=1, source_target_pairs={{0,2},{1,3},{2,0},{3,1},{4,6},{5,7},{6,4},{7,5},{8,10},{9,11},{10,... | collective-permute-start | bytes 7688 | tf_op jit(solution)/shard_map/ppermute | solution.py:236
  364.7 163.4 %collective-permute-start.7 = (bf16[512,3584]{1,0:T(8,128)(2,1)}, bf16[512,3584]{1,0:T(8,128)(2,1)}, u32[]{:S(2)}, u32[]{:S(2)}) collective-permute-start(bf16[512,3584]{1,0:T(8,128)(2,1)} %shard_map.130), channel_id=1, source_target_pairs={{0,2},{1,3},{2,0},{3,1},{4,6},{5,7},{6,4},{7,5},{8,10},{9,11},{10,... | collective-permute-start | bytes 11010056 | tf_op jit(solution)/shard_map/ppermute | solution.py:257
  366.6 161.4 %copy-start.4 = (s32[512]{0:T(512)S(1)}, s32[512]{0:T(512)}, u32[]{:S(2)}) copy-start(s32[512]{0:T(512)} %copy-done.3) | copy-start | bytes 6148
  366.6 161.4 %copy-start.6 = (pred[512]{0:T(512)(128)(4,1)S(1)}, pred[512]{0:T(512)(128)(4,1)}, u32[]{:S(2)}) copy-start(pred[512]{0:T(512)(128)(4,1)} %copy-done.5) | copy-start | bytes 1540
  528.0 4.4 copy-start
  528.0 4.4 copy-start.2
  528.0 4.4 copy-start.8

commit v3 on v2

--- a/solution.py
+++ b/solution.py
@@ -68,18 +68,35 @@
     )(info, x, lid, ag, ag, au, au)
 
 
-def mlp_kernel(rank, sub, wide, resume, final, info_ref, x_ref, lid_ref, lg_ref, lu_ref, wg_ref, wu_ref, bg0_ref, bg1_ref,
+def mlp_kernel(rank, sub, wide, resume, final, begin, info_ref, x_ref, lid_ref, lg_ref, lu_ref, wg_ref, wu_ref, bg0_ref, bg1_ref,
                bu0_ref, bu1_ref, wd_ref, a0_ref, a1_ref, *refs):
     refs = list(refs)
     bd0_ref, bd1_ref = (refs.pop(0), refs.pop(0)) if final else (None, None)
     acc_in, low_in = (refs.pop(0), refs.pop(0)) if resume else (None, None)
     o_ref = refs.pop(0) if final else None
     acc_out, low_out = (None, None) if final else (refs.pop(0), refs.pop(0))
-    acc_ref, low_ref, ld_ref, sems = refs
+    acc_ref, low_ref, ld_ref, sems, ring_ref, ring_sems = refs
     step = pl.program_id(0)
     tok, d = acc_ref.shape
     half = bg0_ref.shape[0]
-    block = wg_ref.shape[1]
+    block = bg0_ref.shape[1]
+    parts = block // sub
+    steps = pl.num_programs(0)
+    base_slot = (step % 2) * parts
+
+    def ring_copies(part, slot):
+        at = pl.ds(pl.multiple_of(begin + part * sub, sub), sub)
+        return [pltpu.make_async_copy(w_ref.at[:, at], ring_ref.at[i, slot], ring_sems.at[i, slot]) for i, w_ref in enumerate((wg_ref, wu_ref))]
+
+    @pl.when(step == 0)
+    def _():
+        for slot in range(2 * parts):
+            for copy in ring_copies(jnp.minimum(slot, steps * parts - 1), slot):
+                copy.start()
+
+    for part in range(parts):
+        for copy in ring_copies(part, base_slot + part):
+            copy.wait()
 
     def move(pairs):
         copies = [pltpu.make_async_copy(src, dst, sems.at[i]) for i, (src, dst) in enumerate(pairs)]
@@ -94,8 +111,9 @@
             partner = jnp.dot(l_ref[split:m, :], b1_ref[:, at], preferred_element_type=F32)
             return (LORA_SCALE * jnp.concatenate([own, partner], axis=0)).astype(BF16).astype(F32)
 
-        def branch(at, w_ref, l_ref, b0_ref, b1_ref):
-            base = jnp.dot(x_ref[:m, :], w_ref[:, at], preferred_element_type=F32)
+        def branch(at, kind, l_ref, b0_ref, b1_ref):
+            weight = ring_ref[kind, base_slot + at.start // sub]
+            base = jnp.dot(x_ref[:m, :], weight, preferred_element_type=F32)
             return base + spread(l_ref, at, b0_ref, b1_ref)
 
         @pl.when(step == 0)
@@ -107,7 +125,7 @@
                 low_ref[:m, :] = jnp.zeros((m, half), F32)
 
         def gate_up(at):
-            return at, branch(at, wg_ref, lg_ref, bg0_ref, bg1_ref), branch(at, wu_ref, lu_ref, bu0_ref, bu1_ref)
+            return at, branch(at, 0, lg_ref, bg0_ref, bg1_ref), branch(at, 1, lu_ref, bu0_ref, bu1_ref)
 
         def add_down(at, gate, up):
             h = (jax.nn.silu(gate) * up).astype(BF16)
@@ -120,6 +138,11 @@
         waiting = None
         for first in range(0, block, sub):
             now = gate_up(slice(first, first + sub))
+            if first + sub == block:
+                for part in range(parts):
+                    following = jnp.minimum((step + 2) * parts + part, steps * parts - 1)
+                    for copy in ring_copies(following, base_slot + part):
+                        copy.start()
             if waiting is not None:
                 add_down(*waiting)
             waiting = now
@@ -146,15 +169,20 @@
 
     per_case(info_ref, tok, body)
 
+    @pl.when(step == steps - 1)
+    def _():
+        for slot in range(2 * parts):
+            for copy in ring_copies(slot, slot):
+                copy.wait()
+
 
 def mlp(info, x, lid, lg, lu, wg, wu, bs, wd, ad, bd, rank, first, stop, sums=None, block=BLOCK, sub=256, wide=512):
     tok, d = x.shape
     low = half = lg.shape[1]
     resume, final = sums is not None, bd is not None
-    spec_w = pl.BlockSpec((d, block), lambda i, info: (0, i + first))
     any_spec = pl.BlockSpec(memory_space=pl.ANY)
     in_specs = [
-        whole((tok, d)), whole((tok, 1)), whole((tok, low)), whole((tok, low)), spec_w, spec_w,
+        whole((tok, d)), whole((tok, 1)), whole((tok, low)), whole((tok, low)), any_spec, any_spec,
         *(pl.BlockSpec((half, block), lambda i, info, off=0 if local else first: (0, i + off)) for _, local in bs),
         pl.BlockSpec((block, d), lambda i, info: (i + first, 0)),
         pl.BlockSpec((half, block), lambda i, info: (info[1], i + first)),
@@ -173,13 +201,13 @@
         args += sums
     width = (stop - first) * block
     return pl.pallas_call(
-        functools.partial(mlp_kernel, rank, sub, wide, resume, final),
+        functools.partial(mlp_kernel, rank, sub, wide, resume, final, first * block),
         grid_spec=pltpu.PrefetchScalarGridSpec(
             num_scalar_prefetch=1,
             grid=(stop - first,),
             in_specs=in_specs,
             out_specs=out_specs,
-            scratch_shapes=[pltpu.VMEM((tok, d), F32), pltpu.VMEM((tok, low), F32), pltpu.VMEM((tok, low), BF16), pltpu.SemaphoreType.DMA((2,))],
+            scratch_shapes=[pltpu.VMEM((tok, d), F32), pltpu.VMEM((tok, low), F32), pltpu.VMEM((tok, low), BF16), pltpu.SemaphoreType.DMA((2,)), pltpu.VMEM((2, 2 * (block // sub), d, sub), BF16), pltpu.SemaphoreType.DMA((2, 2 * (block // sub)))],
         ),
         out_shape=out_shape,
         compiler_params=pltpu.CompilerParams(vmem_limit_bytes=VMEM_LIMIT),
@@ -217,14 +245,18 @@
         lid = adapter_id % per_owner
         token = jnp.arange(tok, dtype=jnp.int32)
         before = token[None, :] < token[:, None]
-        splits, sizes = (jnp.array(column, jnp.int32) for column in zip(*row_cases(tok)))
 
         def place(chosen, hidden):
             own = jnp.sum((chosen & ~partner).astype(jnp.int32))
             other = jnp.sum((chosen & partner).astype(jnp.int32))
-            case = jnp.argmax((own <= splits) & (other <= sizes - splits)).astype(jnp.int32)
+            *rest, last = enumerate(row_cases(tok))
+            case, split = jnp.int32(last[0]), jnp.int32(last[1][0])
+            for index, (first_other, size) in reversed(rest):
+                fits = (own <= first_other) & (other <= size - first_other)
+                case = jnp.where(fits, index, case)
+                split = jnp.where(fits, first_other, split)
             alike = before & chosen[None, :] & (partner[None, :] == partner[:, None])
-            rank_of = jnp.sum(alike.astype(jnp.int32), axis=1) + jnp.where(partner, splits[case], 0)
+            rank_of = jnp.sum(alike.astype(jnp.int32), axis=1) + jnp.where(partner, split, 0)
             hot = (token[:, None] == rank_of[None, :]) & chosen[None, :]
             rows = jnp.dot(hot.astype(BF16), hidden, preferred_element_type=F32).astype(BF16)
             lids = jnp.sum(hot.astype(jnp.int32) * (lid[None, :] + 1), axis=1) - 1

time: 546 us -> 532 us (0.974)
  Pallas kernels: 474 us -> 453 us
  waiting for transfers between devices: 4.29 us -> 20.5 us
  other arithmetic: 10.2 us -> 3.62 us
    pallas_call x3, Pallas kernels: 452 us -> 432 us  [mlp(): pl.pallas_call(functools.partial(mlp_kernel, rank, sub, wide, resume, fin...]
    ppermute x1, waiting for transfers between devices: 4.28 us -> 20.5 us  [device_fn(): recv_lid = lax.ppermute(send_lid, 'data', to_chip)]
  transfers between devices with their start and end apart: 8 -> 8, of which waited for: 1 -> 1; matrix products, arithmetic and copies ran while one was open for 4% -> 3% of each run, Pallas kernels for 48% -> 45%
where the time goes in v3:
time: 532 us; the launch traced here: 527 us
  Pallas kernels  453 us (85%)
  waiting for transfers between devices  20.5 us (4%)
  matrix products  20.2 us (4%)
  local copies, waits for them, and re-layouts  15.3 us (3%)
  between operations  8.13 us (2%)
  starting transfers between devices  6.15 us (1%)
    pallas_call x3, Pallas kernels, mlp(): pl.pallas_call(functools.partial(mlp_kernel, rank, sub, wide, resume, fin...  432 us
    pallas_call x2, Pallas kernels, low_rows(): pl.pallas_call(functools.partial(low_kernel, rank), grid_spec=pltpu.Prefe...  21.6 us
    ppermute x1, waiting for transfers between devices, device_fn(): recv_lid = lax.ppermute(send_lid, 'data', to_chip)  20.5 us
    dot_general x2, matrix products, place(): jnp.dot(hot.astype(BF16), hidden, preferred_element_type=F32).astype(BF16)  11.9 us
  transfers between devices with their start and end apart: 8, of which 1 were waited for; matrix products, arithmetic and copies ran while one was open for 3% of the time, Pallas kernels for 45%

profile of v3, /device:TPU:0, one launch (start us, length us, event | category | flops | bytes accessed | tf_op | source)
XLA Modules:
  0.0 527.1 jit_solution(5170494507991073484)
XLA Ops:
  0.0 0.7 fusion.19
  0.7 0.7 convert_reduce_fusion.4
  1.4 0.0 copy-start.5
  9.1 0.0 copy-start.7
  9.2 0.4 convert_reduce_fusion.1
  9.6 0.0 copy-start.3
  9.6 0.0 copy-start.1
  9.6 5.9 %convolution_convert_fusion.1 = bf16[512,3584]{1,0:T(8,128)(2,1)} fusion(bf16[512,3584]{1,0:T(8,128)(2,1)} %param.11, s32[512]{0:T(512)S(1)} %get-tuple-element.74, pred[512]{0:T(512)(128)(4,1)S(1)} %get-tuple-element.69), kind=kOutput, calls=%fused_computation.2 | convolution fusion | flops 1881407488 | bytes 7342592 | tf_op jit(solution)/shard_map/dot_general | solution.py:261
  15.6 4.8 slice.14
  20.3 0.7 collective-permute-start.1
  21.0 4.8 slice.13
  25.8 0.0 collective-permute-start
  25.8 0.0 copy-done.5
  25.8 0.0 copy-done.3
  25.8 0.5 select_reduce_fusion.1
  26.4 0.9 copy.17.lid_ref
  27.2 0.6 stack.11.info_ref
  27.9 0.0 copy-done.7
  27.9 0.0 copy-done.1
  27.9 5.9 %convolution_convert_fusion.x_ref = bf16[512,3584]{1,0:T(8,128)(2,1)} fusion(bf16[512,3584]{1,0:T(8,128)(2,1)} %param.11, s32[512]{0:T(512)S(1)} %get-tuple-element.73, pred[512]{0:T(512)(128)(4,1)S(1)} %not.7), kind=kOutput, calls=%fused_computation.1 | convolution fusion | flops 1881407488 | bytes 7342592 | tf_op jit(solution)/shard_map/dot_general | solution.py:261
  33.8 10.9 %shard_map.109 = (bf16[512,512]{1,0:T(8,128)(2,1)}, bf16[512,512]{1,0:T(8,128)(2,1)}) custom-call(s32[2]{0:T(128)} %stack.11.info_ref, bf16[512,3584]{1,0:T(8,128)(2,1)} %convolution_convert_fusion.x_ref, s32[512,1]{1,0:T(8,128)} %copy.17.lid_ref, bf16[2048,3584]{1,0:T(8,128)(2,1)} %bitcast.19, bf16[2048,3584]{1,0:T(8,128)(2,1)} %bitcast.20, ...), custom_call_target="tpu_custom_call" | custom-call | flops 3758096384 | bytes 14680064 | tf_op jit(solution)/shard_map/pallas_call | solution.py:57
  44.7 0.0 collective-permute-done.1.bu1_ref
  44.7 0.0 collective-permute-done.bg1_ref
  44.7 0.5 collective-permute-start.2
  45.3 0.1 collective-permute-start.3
  45.3 2.9 collective-permute-start.5
  48.3 0.0 collective-permute-start.4
  48.3 0.6 concatenate.3
  48.9 0.1 collective-permute-start.6
  48.9 0.9 copy.21.lid_ref
  49.8 58.0 %shard_map.110 = (f32[512,3584]{1,0:T(8,128)}, f32[512,512]{1,0:T(8,128)}) custom-call(s32[2]{0:T(128)} %stack.11.info_ref, bf16[512,3584]{1,0:T(8,128)(2,1)} %convolution_convert_fusion.x_ref, s32[512,1]{1,0:T(8,128)} %copy.21.lid_ref, bf16[512,512]{1,0:T(8,128)(2,1)} %get-tuple-element.41.lg_ref, bf16[512,512]{1,0:T(8,128)(2,1)} %get-tuple-element.42.lu_ref, ...), custom_call_target="tpu_custom_call" | custom-call | flops 1000 | bytes 113246208 | tf_op jit(solution)/shard_map/pallas_call | solution.py:203
  107.8 20.5 %collective-permute-done.6 = s32[640]{0:T(1024)} collective-permute-done((s32[640]{0:T(1024)}, s32[640]{0:T(1024)}, u32[]{:S(2)}, u32[]{:S(2)}) %collective-permute-start.6) | collective-permute-done | bytes 2592 | tf_op jit(solution)/shard_map/ppermute | solution.py:268
  128.2 0.0 collective-permute-done.5.x_ref
  128.2 1.2 slice.15
  129.4 0.7 slice.16
  130.1 0.9 copy.20.lid_ref
  131.0 1.2 pad_add_fusion.info_ref
  132.2 10.7 %shard_map.111 = (bf16[512,512]{1,0:T(8,128)(2,1)}, bf16[512,512]{1,0:T(8,128)(2,1)}) custom-call(s32[2]{0:T(128)} %pad_add_fusion.info_ref, bf16[512,3584]{1,0:T(8,128)(2,1)} %collective-permute-done.5.x_ref, s32[512,1]{1,0:T(8,128)} %copy.20.lid_ref, bf16[2048,3584]{1,0:T(8,128)(2,1)} %bitcast.21, bf16[2048,3584]{1,0:T(8,128)(2,1)} %bitcast.22, ...), custom_call_target="tpu_custom_call" | custom-call | flops 3758096384 | bytes 14680064 | tf_op jit(solution)/shard_map/pallas_call | solution.py:57
  142.9 0.0 collective-permute-done.4.refs_1_
  142.9 0.0 collective-permute-done.2.bg1_ref
  142.9 0.0 collective-permute-done.3.bu1_ref
  143.0 215.0 %shard_map.112 = bf16[512,3584]{1,0:T(8,128)(2,1)} custom-call(s32[2]{0:T(128)} %pad_add_fusion.info_ref, bf16[512,3584]{1,0:T(8,128)(2,1)} %collective-permute-done.5.x_ref, s32[512,1]{1,0:T(8,128)} %copy.20.lid_ref, bf16[512,512]{1,0:T(8,128)(2,1)} %get-tuple-element.55.lg_ref, bf16[512,512]{1,0:T(8,128)(2,1)} %get-tuple-element.56.lu_ref, ...), custom_call_target="tpu_custom_call" | custom-call | flops 238370684928 | bytes 465567744 | tf_op jit(solution)/shard_map/pallas_call | solution.py:203
  358.0 1.8 collective-permute-start.7
  359.8 0.0 copy-start.4
  359.8 0.0 copy-start.6
  359.8 158.7 %shard_map.113 = bf16[512,3584]{1,0:T(8,128)(2,1)} custom-call(s32[2]{0:T(128)} %stack.11.info_ref, bf16[512,3584]{1,0:T(8,128)(2,1)} %convolution_convert_fusion.x_ref, s32[512,1]{1,0:T(8,128)} %copy.21.lid_ref, bf16[512,512]{1,0:T(8,128)(2,1)} %get-tuple-element.41.lg_ref, bf16[512,512]{1,0:T(8,128)(2,1)} %get-tuple-element.42.lu_ref, ...), custom_call_target="tpu_custom_call" | custom-call | flops 180388626432 | bytes 352321536 | tf_op jit(solution)/shard_map/pallas_call | solution.py:203
  518.6 0.0 copy-start
  518.6 0.0 copy-start.2
  518.6 0.0 copy-start.8
  518.6 0.0 collective-permute-done.7
  518.6 0.0 copy-done.4
  518.6 0.0 copy-done.6
  518.6 4.3 fusion.6
  522.9 0.0 copy-done
  522.9 0.0 copy-done.2
  522.9 0.0 copy-done.8
  523.0 4.0 add_convert_fusion
  (4 shorter events, 0.0 us)
Async XLA Ops:
  1.4 24.4 %copy-start.5 = (pred[512]{0:T(512)(128)(4,1)}, pred[512]{0:T(512)(128)(4,1)S(1)}, u32[]{:S(2)}) copy-start(pred[512]{0:T(512)(128)(4,1)S(1)} %get-tuple-element.69) | copy-start | bytes 1540
  9.1 18.7 %copy-start.7 = (pred[512]{0:T(512)(128)(4,1)}, pred[512]{0:T(512)(128)(4,1)S(1)}, u32[]{:S(2)}) copy-start(pred[512]{0:T(512)(128)(4,1)S(1)} %not.7) | copy-start | bytes 1540
  9.6 16.2 %copy-start.3 = (s32[512]{0:T(512)}, s32[512]{0:T(512)S(1)}, u32[]{:S(2)}) copy-start(s32[512]{0:T(512)S(1)} %get-tuple-element.74) | copy-start | bytes 6148
  9.6 18.3 %copy-start.1 = (s32[512]{0:T(512)}, s32[512]{0:T(512)S(1)}, u32[]{:S(2)}) copy-start(s32[512]{0:T(512)S(1)} %get-tuple-element.73) | copy-start | bytes 6148
  20.3 24.4 %collective-permute-start.1 = (bf16[512,4608]{1,0:T(8,128)(2,1)}, bf16[512,4608]{1,0:T(8,128)(2,1)}, u32[]{:S(2)}, u32[]{:S(2)}) collective-permute-start(bf16[512,4608]{1,0:T(8,128)(2,1)} %slice.14), channel_id=1, source_target_pairs={{0,1},{1,0},{2,3},{3,2},{4,5},{5,4},{6,7},{7,6},{8,9},{9,8},{10,11... | collective-permute-start | bytes 14155784 | tf_op jit(solution)/shard_map/ppermute | solution.py:270
  25.8 18.9 %collective-permute-start = (bf16[512,4608]{1,0:T(8,128)(2,1)}, bf16[512,4608]{1,0:T(8,128)(2,1)}, u32[]{:S(2)}, u32[]{:S(2)}) collective-permute-start(bf16[512,4608]{1,0:T(8,128)(2,1)} %slice.13), channel_id=1, source_target_pairs={{0,1},{1,0},{2,3},{3,2},{4,5},{5,4},{6,7},{7,6},{8,9},{9,8},{10,11... | collective-permute-start | bytes 14155784 | tf_op jit(solution)/shard_map/ppermute | solution.py:270
  44.7 98.2 %collective-permute-start.2 = (bf16[512,18944]{1,0:T(8,128)(2,1)}, bf16[512,18944]{1,0:T(8,128)(2,1)}, u32[]{:S(2)}, u32[]{:S(2)}) collective-permute-start(bf16[512,18944]{1,0:T(8,128)(2,1)} %bitcast.28), channel_id=1, source_target_pairs={{0,1},{1,0},{2,3},{3,2},{4,5},{5,4},{6,7},{7,6},{8,9},{9,8},{10,11... | collective-permute-start | bytes 58195976 | tf_op jit(solution)/shard_map/ppermute | solution.py:281
  45.3 97.7 %collective-permute-start.3 = (bf16[512,18944]{1,0:T(8,128)(2,1)}, bf16[512,18944]{1,0:T(8,128)(2,1)}, u32[]{:S(2)}, u32[]{:S(2)}) collective-permute-start(bf16[512,18944]{1,0:T(8,128)(2,1)} %bitcast.33), channel_id=1, source_target_pairs={{0,1},{1,0},{2,3},{3,2},{4,5},{5,4},{6,7},{7,6},{8,9},{9,8},{10,11... | collective-permute-start | bytes 58195976 | tf_op jit(solution)/shard_map/ppermute | solution.py:281
  45.3 82.9 %collective-permute-start.5 = (bf16[512,3584]{1,0:T(8,128)(2,1)}, bf16[512,3584]{1,0:T(8,128)(2,1)}, u32[]{:S(2)}, u32[]{:S(2)}) collective-permute-start(bf16[512,3584]{1,0:T(8,128)(2,1)} %convolution_convert_fusion.1), channel_id=1, source_target_pairs={{0,2},{1,3},{2,0},{3,1},{4,6},{5,7},{6,4},{7,5},{8,10},{9,11},{10,... | collective-permute-start | bytes 11010056 | tf_op jit(solution)/shard_map/ppermute | solution.py:267
  48.3 94.7 %collective-permute-start.4 = (bf16[512,3584]{1,0:T(8,128)(2,1)}, bf16[512,3584]{1,0:T(8,128)(2,1)}, u32[]{:S(2)}, u32[]{:S(2)}) collective-permute-start(bf16[512,3584]{1,0:T(8,128)(2,1)} %bitcast.40), channel_id=1, source_target_pairs={{0,1},{1,0},{2,3},{3,2},{4,5},{5,4},{6,7},{7,6},{8,9},{9,8},{10,11... | collective-permute-start | bytes 11010056 | tf_op jit(solution)/shard_map/ppermute | solution.py:281
  48.9 79.4 %collective-permute-start.6 = (s32[640]{0:T(1024)}, s32[640]{0:T(1024)}, u32[]{:S(2)}, u32[]{:S(2)}) collective-permute-start(s32[640]{0:T(1024)} %concatenate.3), channel_id=1, source_target_pairs={{0,2},{1,3},{2,0},{3,1},{4,6},{5,7},{6,4},{7,5},{8,10},{9,11},{10,... | collective-permute-start | bytes 7688 | tf_op jit(solution)/shard_map/ppermute | solution.py:268
  358.0 160.6 %collective-permute-start.7 = (bf16[512,3584]{1,0:T(8,128)(2,1)}, bf16[512,3584]{1,0:T(8,128)(2,1)}, u32[]{:S(2)}, u32[]{:S(2)}) collective-permute-start(bf16[512,3584]{1,0:T(8,128)(2,1)} %shard_map.112), channel_id=1, source_target_pairs={{0,2},{1,3},{2,0},{3,1},{4,6},{5,7},{6,4},{7,5},{8,10},{9,11},{10,... | collective-permute-start | bytes 11010056 | tf_op jit(solution)/shard_map/ppermute | solution.py:289
  359.8 158.8 %copy-start.4 = (s32[512]{0:T(512)S(1)}, s32[512]{0:T(512)}, u32[]{:S(2)}) copy-start(s32[512]{0:T(512)} %copy-done.3) | copy-start | bytes 6148
  359.8 158.8 %copy-start.6 = (pred[512]{0:T(512)(128)(4,1)S(1)}, pred[512]{0:T(512)(128)(4,1)}, u32[]{:S(2)}) copy-start(pred[512]{0:T(512)(128)(4,1)} %copy-done.5) | copy-start | bytes 1540
  518.6 4.4 copy-start
  518.6 4.4 copy-start.2
  518.6 4.4 copy-start.8
